TPU v7x, 8 devices: a whole 2x2x1 slice. The times are simulated.
8 devices in a mesh: replica: 4 (over z, y, x), data: 2 (over core).
Axes of the slice: x: 2, y: 2, z: 1, core: 2. Of those that a mesh axis runs over, the one named last changes fastest.
Arguments:
- w_one: bfloat16 [3, 1920, 7680], replicated
- w_two: bfloat16 [3, 7680, 1920], replicated
- x_in: bfloat16 [24, 2, 64, 1920], P(('replica', 'data'))
- dy_in: bfloat16 [24, 2, 64, 1920], P(('replica', 'data'))
Outputs:
- output 1: bfloat16 [3, 1920, 7680], replicated
- output 2: bfloat16 [3, 7680, 1920], replicated
- output 3: bfloat16 [24, 2, 64, 1920], P(('replica', 'data'))
All inputs are finite; a program needn't handle non-finite values.
Results may differ from a plain program's by a relative error of at most 0.0193242.
Values are sent between devices in bfloat16 or wider.
A program may use at most 1.5 GiB of HBM per device.

v0:
```python
import jax
import jax.numpy as jnp
from jax import lax
from jax.sharding import PartitionSpec as P


def gelu_tanh(value):
    return jax.nn.gelu(value, approximate=True)


def forward_saved(w_one, w_two, tokens):
    layers = w_one.shape[0]
    saved_acts = []
    hidden = tokens
    for layer in range(layers):
        pre_act = jnp.dot(hidden, w_one[layer], preferred_element_type=jnp.float32).astype(jnp.bfloat16)
        gelu_out = gelu_tanh(pre_act.astype(jnp.float32)).astype(jnp.bfloat16)
        saved_acts.append((hidden, pre_act, gelu_out))
        if layer < layers - 1:
            hidden = (hidden.astype(jnp.float32) + jnp.dot(gelu_out, w_two[layer], preferred_element_type=jnp.float32)).astype(jnp.bfloat16)
    return saved_acts


def layer_backward(w_up, w_down, saved_layer, upstream):
    hidden, pre_act, gelu_out = saved_layer
    grad_b = upstream.astype(jnp.bfloat16)
    d_two = jnp.einsum("tf,tm->fm", gelu_out, grad_b, preferred_element_type=jnp.float32)
    d_act = jnp.einsum("tm,fm->tf", grad_b, w_down, preferred_element_type=jnp.float32)
    d_pre = jax.vjp(gelu_tanh, pre_act.astype(jnp.float32))[1](d_act)[0].astype(jnp.bfloat16)
    d_one = jnp.einsum("tm,tf->mf", hidden, d_pre, preferred_element_type=jnp.float32)
    new_upstream = upstream + jnp.einsum("tf,mf->tm", d_pre, w_up, preferred_element_type=jnp.float32)
    return d_one, d_two, new_upstream


def reduce_grads(accumulators):
    stacked = jnp.stack([part_acc.astype(jnp.bfloat16) for part_acc in accumulators])
    grad_shard = lax.psum_scatter(stacked, "data", scatter_dimension=1, tiled=True)
    grad_shard = lax.psum(grad_shard, "replica")
    return lax.all_gather(grad_shard, "data", axis=1, tiled=True)


def solution(mesh):
    batch_spec = P(("replica", "data"))

    def per_device(w_one, w_two, x_loc, dy_loc):
        micro_count, seq_count, length, model_width = x_loc.shape
        layers = w_one.shape[0]
        acc_one = [None] * layers
        acc_two = [None] * layers
        dx_parts = []
        for micro_idx in range(micro_count):
            saved_acts = forward_saved(w_one, w_two, x_loc[micro_idx].reshape(seq_count * length, model_width))
            upstream = dy_loc[micro_idx].reshape(seq_count * length, model_width).astype(jnp.float32)
            for layer in reversed(range(layers)):
                d_one, d_two, upstream = layer_backward(w_one[layer], w_two[layer], saved_acts[layer], upstream)
                if micro_idx > 0:
                    d_one = acc_one[layer] + d_one
                    d_two = acc_two[layer] + d_two
                acc_one[layer] = d_one
                acc_two[layer] = d_two
            dx_parts.append(upstream.astype(jnp.bfloat16).reshape(seq_count, length, model_width))
        return reduce_grads(acc_one), reduce_grads(acc_two), jnp.stack(dx_parts)

    return jax.shard_map(per_device, mesh=mesh, in_specs=(P(), P(), batch_spec, batch_spec), out_specs=(P(), P(), batch_spec), check_vma=False)
```

profile of v0, /device:TPU:0, one launch (start us, length us, event | category | flops | bytes accessed | tf_op | source)
XLA Modules:
  0.0 3517.7 jit_solution(10911874095846633079)
XLA Ops:
  7.2 2.5 fusion.355
  10.8 11.9 fusion.108
  24.7 12.3 fusion.309
  37.0 11.8 fusion.126
  48.7 13.0 fusion.300
  61.8 14.0 fusion.144
  75.7 15.5 fusion.179
  92.6 13.9 fusion.276
  106.5 15.0 fusion.172
  121.5 15.2 fusion.258
  136.8 21.1 fusion.358
  157.9 12.0 fusion.114
  171.7 11.5 fusion.306
  183.2 11.9 fusion.132
  195.2 12.9 fusion.297
  208.1 13.9 fusion.150
  222.1 15.7 fusion.200
  237.7 13.9 fusion.279
  251.7 15.0 fusion.193
  266.7 15.2 fusion.261
  281.9 21.1 fusion.359
  303.1 22.4 fusion.361
  325.5 22.3 fusion.360
  347.8 11.7 fusion.120
  361.5 11.5 fusion.303
  373.0 11.9 fusion.138
  385.0 12.9 fusion.294
  397.9 13.9 fusion.156
  411.8 15.4 fusion.221
  427.2 14.6 fusion.282
  441.8 16.1 fusion.214
  457.9 15.4 fusion.264
  473.3 14.8 fusion.165
  488.1 21.2 fusion.356
  509.3 16.3 fusion.186
  525.6 23.1 fusion.357
  548.7 15.2 fusion.207
  564.0 49.0 %fusion.67 = bf16[1,1920,7680]{1,2,0:T(8,128)(2,1)} fusion(bf16[128,1920]{1,0:T(8,128)(2,1)S(1)} %copy-done.58, bf16[128,7680]{1,0:T(8,128)(2,1)} %fusion.214, f32[1920,7680]{0,1:T(8,128)} %fusion.358, f32[1920,7680]{0,1:T(8,128)} %fusion.359), kind=kOutput, calls=%fused_computation.75 | convolution fusion | flops 3819110400 | bytes 149913600 | tf_op jit(solution)/shard_map/tm,tf->mf/dot_general | solution.py:30
  613.0 48.3 %fusion.68 = bf16[1,1920,7680]{1,2,0:T(8,128)(2,1)} fusion(bf16[128,1920]{1,0:T(8,128)(2,1)S(1)} %copy-done.56, bf16[128,7680]{1,0:T(8,128)(2,1)} %copy-done.27, f32[1920,7680]{0,1:T(8,128)} %fusion.360, f32[1920,7680]{0,1:T(8,128)} %fusion.361), kind=kOutput, calls=%fused_computation.76 | convolution fusion | flops 3819110400 | bytes 149913600 | tf_op jit(solution)/shard_map/tm,tf->mf/dot_general | solution.py:30
  661.3 47.4 %fusion.66 = bf16[1,1920,7680]{1,2,0:T(8,128)(2,1)} fusion(bf16[128,7680]{1,0:T(8,128)(2,1)S(1)} %fusion.207, bf16[128,1920]{1,0:T(8,128)(2,1)S(1)} %bitcast.251, f32[7680,1920]{1,0:T(8,128)} %fusion.356, f32[7680,1920]{1,0:T(8,128)} %fusion.357), kind=kOutput, calls=%fused_computation.74 | convolution fusion | flops 3819110400 | bytes 149913600 | tf_op jit(solution)/shard_map/tm,tf->mf/dot_general | solution.py:30
  708.7 58.3 %pad_maximum_fusion = bf16[3,1920,7680]{1,2,0:T(8,128)(2,1)} fusion(bf16[1,1920,7680]{1,2,0:T(8,128)(2,1)} %fusion.68, bf16[1,1920,7680]{1,2,0:T(8,128)(2,1)} %fusion.67, bf16[1,1920,7680]{1,2,0:T(8,128)(2,1)} %fusion.66), kind=kLoop, calls=%fused_computation | loop fusion | flops 88473600 | bytes 176947200 | tf_op jit(solution)/shard_map/stack | solution.py:36
  767.0 186.4 %copy.27 = bf16[3,1920,7680]{2,0,1:T(4,128)(2,1)} copy(bf16[3,1920,7680]{1,2,0:T(8,128)(2,1)} %pad_maximum_fusion) | data formatting | bytes 176947200
  953.4 66.9 %copy.29 = bf16[240,8,3,7680]{3,1,2,0:T(8,128)(2,1)} copy(bf16[240,8,3,7680]{3,2,1,0:T(4,128)(2,1)} %bitcast.26) | data formatting | bytes 176947200
  1021.3 45.8 %fusion.312 = f32[7680,1920]{1,0:T(8,128)} fusion(bf16[128,1920]{1,0:T(8,128)(2,1)S(1)} %bitcast.266, f32[128,7680]{1,0:T(8,128)} %fusion.144), kind=kOutput, calls=%fused_computation.245 | convolution fusion | flops 3783720960 | bytes 63406080 | tf_op jit(solution)/shard_map/tf,tm->fm/dot_general | solution.py:27
  1067.1 42.1 %fusion.313 = f32[7680,1920]{1,0:T(8,128)} fusion(bf16[128,1920]{1,0:T(8,128)(2,1)S(1)} %bitcast.263, f32[128,7680]{1,0:T(8,128)S(1)} %copy-done.9), kind=kOutput, calls=%fused_computation.246 | convolution fusion | flops 3783720960 | bytes 63406080 | tf_op jit(solution)/shard_map/tf,tm->fm/dot_general | solution.py:27
  1109.2 21.2 fusion.330
  1130.4 21.3 fusion.336
  1151.7 21.4 fusion.333
  1173.1 21.3 fusion.339
  1194.5 48.6 %fusion.71 = bf16[1,7680,1920]{2,1,0:T(8,128)(2,1)} fusion(bf16[128,1920]{1,0:T(8,128)(2,1)S(1)} %bitcast.254, f32[7680,1920]{1,0:T(8,128)} %fusion.312, f32[7680,1920]{1,0:T(8,128)} %fusion.313, f32[128,7680]{1,0:T(8,128)} %fusion.156), kind=kOutput, calls=%fused_computation.79 | convolution fusion | flops 3827957760 | bytes 151879680 | tf_op jit(solution)/shard_map/tf,tm->fm/dot_general | solution.py:27
  1243.1 48.7 %fusion.69 = bf16[1,7680,1920]{2,1,0:T(8,128)(2,1)} fusion(f32[7680,1920]{1,0:T(8,128)} %fusion.336, f32[7680,1920]{1,0:T(8,128)} %fusion.330, f32[128,1920]{1,0:T(8,128)S(1)} %copy-done.44, f32[128,7680]{1,0:T(8,128)} %copy-done.11), kind=kOutput, calls=%fused_computation.77 | convolution fusion | flops 3828203520 | bytes 152371200 | tf_op jit(solution)/shard_map/tf,tm->fm/dot_general | solution.py:27
  1291.8 48.6 %fusion.70 = bf16[1,7680,1920]{2,1,0:T(8,128)(2,1)} fusion(f32[7680,1920]{1,0:T(8,128)} %fusion.339, f32[7680,1920]{1,0:T(8,128)} %fusion.333, f32[128,1920]{1,0:T(8,128)S(1)} %copy-done.47, f32[128,7680]{1,0:T(8,128)} %copy-done.10), kind=kOutput, calls=%fused_computation.78 | convolution fusion | flops 3828203520 | bytes 152371200 | tf_op jit(solution)/shard_map/tf,tm->fm/dot_general | solution.py:27
  1340.4 58.3 %pad_maximum_fusion.1 = bf16[3,7680,1920]{2,1,0:T(8,128)(2,1)} fusion(bf16[1,7680,1920]{2,1,0:T(8,128)(2,1)} %fusion.71, bf16[1,7680,1920]{2,1,0:T(8,128)(2,1)} %fusion.70, bf16[1,7680,1920]{2,1,0:T(8,128)(2,1)} %fusion.69), kind=kLoop, calls=%fused_computation.1 | loop fusion | flops 88473600 | bytes 176947200 | tf_op jit(solution)/shard_map/stack | solution.py:36
  1398.8 93.2 %reshape.7 = bf16[960,3,7680]{2,1,0:T(4,128)(2,1)} reshape(bf16[960,23040]{1,0:T(8,128)(2,1)} %reduce-scatter.7.cloned.1.call-done) | data formatting | bytes 88473600
  1492.0 89.2 %copy.28 = bf16[3,960,7680]{1,2,0:T(8,128)(2,1)} copy(bf16[3,960,7680]{2,0,1:T(4,128)(2,1)} %bitcast.248) | data formatting | bytes 88473600
  1581.3 1505.9 %all-reduce.3.cloned.1.call-done = (bf16[3,960,7680]{1,2,0:T(8,128)(2,1)}, bf16[3,3840,1920]{2,1,0:T(8,128)(2,1)}) async-done(((bf16[3,960,7680]{1,2,0:T(8,128)(2,1)}, bf16[3,3840,1920]{2,1,0:T(8,128)(2,1)}), (bf16[3,960,7680]{1,2,0:T(8,128)(2,1)}, bf16[3,3840,1920]{2,1,0:T(8,128)(2,1)})) %all-reduce.3.cloned.1.call-update) | async-done | bytes 88473616 | tf_op jit(solution)/shard_map/psum | solution.py:38
  3087.2 60.1 %copy.20 = bf16[3,960,7680]{2,1,0:T(8,128)(2,1)} copy(bf16[3,960,7680]{1,2,0:T(8,128)(2,1)} %get-tuple-element.6) | data formatting | bytes 88473600 | tf_op jit(solution)/shard_map/psum | solution.py:38
  3149.2 20.2 fusion.291
  3169.5 24.2 fusion.288
  3193.8 20.9 fusion.285
  3216.0 54.9 %all-gather.3.cloned.1.call-done = bf16[3,1920,7680]{2,1,0:T(8,128)(2,1)} async-done(((bf16[3,960,7680]{2,1,0:T(8,128)(2,1)}), bf16[3,1920,7680]{2,1,0:T(8,128)(2,1)}) %all-gather.3.cloned.1.call-update) | async-done | bytes 88473616 | tf_op jit(solution)/shard_map/all_gather | solution.py:39
  3270.9 123.6 %all-gather.5.cloned.1.call-done = bf16[3,7680,1920]{2,1,0:T(8,128)(2,1)} async-done(((bf16[3,3840,1920]{2,1,0:T(8,128)(2,1)}), bf16[3,7680,1920]{2,1,0:T(8,128)(2,1)}) %all-gather.5.cloned.1.call-update) | async-done | bytes 88473616 | tf_op jit(solution)/shard_map/all_gather | solution.py:39
  3394.5 58.3 %copy.34 = bf16[3,1920,7680]{2,1,0:T(8,128)(2,1)} copy(bf16[3,1920,7680]{2,1,0:T(8,128)(2,1)} %all-gather.3.cloned.1.call-done) | data formatting | bytes 176947200
  3452.8 58.1 %copy.35 = bf16[3,7680,1920]{2,1,0:T(8,128)(2,1)} copy(bf16[3,7680,1920]{2,1,0:T(8,128)(2,1)} %all-gather.5.cloned.1.call-done) | data formatting | bytes 176947200
  (132 shorter events, 12.6 us)
Async XLA Ops:
  7.2 2.5 copy-start.32
  7.2 1391.6 %reduce-scatter.7.cloned.1.call-start = ((), (), s32[]{:S(2)}) async-start(), calls=%async_computation.5 | async-start | bytes 132710400
  9.7 13.1 copy-start.23
  10.8 80.5 %copy-start.30 = (bf16[1,2,64,1920]{3,2,1,0:T(8,128)(2,1)}, bf16[1,2,64,1920]{3,2,1,0:T(8,128)(2,1)S(1)}, u32[]{:S(2)}) copy-start(bf16[1,2,64,1920]{3,2,1,0:T(8,128)(2,1)S(1)} %get-tuple-element.9) | copy-start | bytes 1474564
  22.8 1.9 copy-start.2
  48.7 57.8 %copy-start = (f32[128,7680]{1,0:T(8,128)}, f32[128,7680]{1,0:T(8,128)S(1)}, u32[]{:S(2)}) copy-start(f32[128,7680]{1,0:T(8,128)S(1)} %fusion.126) | copy-start | bytes 11796484
  61.8 14.0 copy-start.48
  91.3 1.3 copy-start.25
  106.5 15.0 copy-start.39
  121.5 15.3 copy-start.52
  136.8 21.2 copy-start.21
  169.9 1.9 copy-start.7
  183.2 12.0 copy-start.53
  195.2 56.5 %copy-start.5 = (f32[128,7680]{1,0:T(8,128)}, f32[128,7680]{1,0:T(8,128)S(1)}, u32[]{:S(2)}) copy-start(f32[128,7680]{1,0:T(8,128)S(1)} %fusion.132) | copy-start | bytes 11796484
  208.1 14.0 copy-start.50
  208.1 14.0 copy-start.28
  251.7 15.0 copy-start.41
  266.7 15.3 copy-start.54
  281.9 21.1 copy-start.51
  303.1 22.4 copy-start.26
  303.1 22.5 copy-start.49
  325.5 22.3 copy-start.17
  359.5 2.0 copy-start.11
  373.0 12.0 copy-start.57
  385.0 56.8 %copy-start.10 = (f32[128,7680]{1,0:T(8,128)}, f32[128,7680]{1,0:T(8,128)S(1)}, u32[]{:S(2)}) copy-start(f32[128,7680]{1,0:T(8,128)S(1)} %fusion.138) | copy-start | bytes 11796484
  397.9 13.9 copy-start.55
  397.9 13.9 copy-start.19
  427.2 14.6 copy-start.27
  441.8 16.1 copy-start.46
  457.9 15.4 copy-start.3
  457.9 15.4 copy-start.33
  473.3 14.8 copy-start.24
  488.1 21.2 copy-start.12
  488.1 21.2 copy-start.36
  509.3 16.3 copy-start.22
  525.6 23.1 copy-start.43
  548.7 15.2 copy-start.58
  564.0 97.3 %copy-start.15 = (bf16[128,7680]{1,0:T(8,128)(2,1)}, bf16[128,7680]{1,0:T(8,128)(2,1)S(1)}, u32[]{:S(2)}) copy-start(bf16[128,7680]{1,0:T(8,128)(2,1)S(1)} %fusion.207) | copy-start | bytes 5898244
  564.0 49.0 %copy-start.56 = (bf16[128,1920]{1,0:T(8,128)(2,1)S(1)}, bf16[128,1920]{1,0:T(8,128)(2,1)}, u32[]{:S(2)}) copy-start(bf16[128,1920]{1,0:T(8,128)(2,1)} %copy-done.55) | copy-start | bytes 1474564
  613.0 48.3 %copy-start.18 = (bf16[1,2,64,1920]{3,2,1,0:T(8,128)(2,1)S(1)}, bf16[1,2,64,1920]{3,2,1,0:T(8,128)(2,1)}, u32[]{:S(2)}) copy-start(bf16[1,2,64,1920]{3,2,1,0:T(8,128)(2,1)} %get-tuple-element.13) | copy-start | bytes 1474564
  1020.2 1.0 copy-start.31
  1020.3 46.8 %copy-start.29 = (bf16[1,2,64,1920]{3,2,1,0:T(8,128)(2,1)S(1)}, bf16[1,2,64,1920]{3,2,1,0:T(8,128)(2,1)}, u32[]{:S(2)}) copy-start(bf16[1,2,64,1920]{3,2,1,0:T(8,128)(2,1)} %get-tuple-element.8) | copy-start | bytes 1474564
  1020.3 560.9 %reduce-scatter.5.cloned.1.call-start = ((), (), s32[]{:S(2)}) async-start(), calls=%async_computation.3 | async-start | bytes 132710400 | tf_op jit(solution)/shard_map/reduce_scatter | solution.py:37
  1021.3 45.8 %copy-start.9 = (f32[128,7680]{1,0:T(8,128)S(1)}, f32[128,7680]{1,0:T(8,128)}, u32[]{:S(2)}) copy-start(f32[128,7680]{1,0:T(8,128)} %fusion.150) | copy-start | bytes 11796484
  1067.1 42.1 %copy-start.8 = (f32[128,7680]{1,0:T(8,128)S(1)}, f32[128,7680]{1,0:T(8,128)}, u32[]{:S(2)}) copy-start(f32[128,7680]{1,0:T(8,128)} %copy-done.7) | copy-start | bytes 11796484
  1067.1 42.1 %copy-start.37 = (f32[128,1920]{1,0:T(8,128)S(1)}, f32[128,1920]{1,0:T(8,128)}, u32[]{:S(2)}) copy-start(f32[128,1920]{1,0:T(8,128)} %fusion.261) | copy-start | bytes 2949124
  1109.2 21.2 copy-start.4
  1109.2 21.2 copy-start.34
  1130.4 21.3 copy-start.6
  1130.4 21.3 copy-start.42
  1151.7 21.4 copy-start.1
  1151.7 21.4 copy-start.40
  1173.1 21.3 copy-start.20
  1194.5 48.6 %copy-start.44 = (f32[128,1920]{1,0:T(8,128)S(1)}, f32[128,1920]{1,0:T(8,128)}, u32[]{:S(2)}) copy-start(f32[128,1920]{1,0:T(8,128)} %fusion.264) | copy-start | bytes 2949124
  1243.1 48.7 %copy-start.47 = (f32[128,1920]{1,0:T(8,128)S(1)}, f32[128,1920]{1,0:T(8,128)}, u32[]{:S(2)}) copy-start(f32[128,1920]{1,0:T(8,128)} %copy-done.46) | copy-start | bytes 2949124
  1398.7 1688.5 %all-reduce.3.cloned.1.call-start = ((), (), s32[]{:S(2)}) async-start(), calls=%async_computation.6 | async-start | bytes 182845440 | tf_op jit(solution)/shard_map/psum | solution.py:38
  1581.2 1689.7 %all-gather.3.cloned.1.call-start = ((), (), s32[]{:S(2)}) async-start(), calls=%async_computation.2 | async-start | bytes 132710400 | tf_op jit(solution)/shard_map/all_gather | solution.py:39
  3147.4 247.2 %all-gather.5.cloned.1.call-start = ((), (), s32[]{:S(2)}) async-start(), calls=%async_computation.4 | async-start | bytes 132710400 | tf_op jit(solution)/shard_map/all_gather | solution.py:39
  3147.4 1.5 copy-start.13
  3147.4 1.8 copy-start.35
  3149.2 20.2 copy-start.14
  3149.2 20.2 copy-start.38
  3169.5 24.3 copy-start.16
  3169.5 24.3 copy-start.45
Sparse Core Ops, SparseCore 0:
  1020.4 88.7 reduce-scatter.6
  1398.8 88.7 reduce-scatter.4
  1581.4 1505.8 all-reduce.2
  3147.5 123.3 all-gather.2
  3272.3 122.2 all-gather.4
where the time goes:
time: 3540 us; the launch traced here: 3520 us
  waiting for transfers between devices  1690 us (48%)
  matrix products  1070 us (30%)
  local copies, waits for them, and re-layouts  625 us (18%)
  other arithmetic  118 us (3%)
    psum x1, waiting for transfers between devices, reduce_grads(): grad_shard = lax.psum(grad_shard, 'replica')  1510 us
    unnamed x124, local copies, waits for them, and re-layouts  561 us
    dot_general x9, matrix products, layer_backward(): jnp.einsum('tf,tm->fm', gelu_out, grad_b, preferred_element_type=jnp.floa...  319 us
    dot_general x9, matrix products, layer_backward(): jnp.einsum('tm,tf->mf', hidden, d_pre, preferred_element_type=jnp.float32)  276 us
    all_gather x2, waiting for transfers between devices, reduce_grads(): return lax.all_gather(grad_shard, 'data', axis=1, tiled=True)  179 us
    dot_general x9, matrix products, layer_backward(): jnp.einsum('tf,mf->tm', d_pre, w_up, preferred_element_type=jnp.float32)  154 us
    dot_general x9, matrix products, layer_backward(): jnp.einsum('tm,fm->tf', grad_b, w_down, preferred_element_type=jnp.float32)  139 us
    another operation x2, other arithmetic, reduce_grads(): jnp.stack([part_acc.astype(jnp.bfloat16) for part_acc in accumulators])  117 us
  transfers between devices with their start and end apart: 5, of which 3 were waited for; matrix products, arithmetic and copies ran while one was open for 18% of the time, Pallas kernels for 0%

commit v1 on v0

v1 whole, which is shorter than its diff:
```python
import jax
import jax.numpy as jnp
from jax import lax
from jax.sharding import PartitionSpec as P


SWAP = ((0, 1), (1, 0))


def gelu_tanh(value):
    return jax.nn.gelu(value, approximate=True)


def swap_cores(value):
    return lax.ppermute(value, "data", SWAP)


def solution(mesh):
    batch_spec = P(("replica", "data"))

    def per_device(w_one, w_two, x_loc, dy_loc):
        layers, model, hidden = w_one.shape
        per = hidden // model // 2
        core = lax.axis_index("data")
        tokens = x_loc.reshape(-1, model)

        def cut(wide, who, axis=1):
            return lax.dynamic_slice_in_dim(wide, who * per * model, per * model, axis)

        def cut_top(w, who, axis):
            start, size = [top, 0, 0], [1, *w.shape[1:]]
            start[axis], size[axis] = who * per * model, per * model
            return lax.dynamic_slice(w, start, size)[0]

        def up(h, w):
            u = jnp.dot(h, w, preferred_element_type=jnp.float32).astype(jnp.bfloat16)
            return u, gelu_tanh(u.astype(jnp.float32)).astype(jnp.bfloat16)

        def grad_one(h, du):
            return jnp.einsum("tm,tf->mf", h, du, preferred_element_type=jnp.float32)

        def grad_two(a, gb):
            return jnp.einsum("tf,tm->fm", a, gb, preferred_element_type=jnp.float32)

        def grad_pre(gb, w, u):
            d_act = jnp.einsum("tm,fm->tf", gb, w, preferred_element_type=jnp.float32)
            return jax.vjp(gelu_tanh, u.astype(jnp.float32))[1](d_act)[0].astype(jnp.bfloat16)

        def grad_in(du, w):
            return jnp.einsum("tf,mf->tm", du, w, preferred_element_type=jnp.float32)

        def part(wide, b):
            return lax.slice_in_dim(wide, b * model, (b + 1) * model, axis=1)

        def own_blocks(dot, away, here):
            got = [swap_cores(dot(part(away, b)).astype(jnp.bfloat16)) for b in range(per)]
            return [(dot(part(here, b)) + got[b].astype(jnp.float32)).astype(jnp.bfloat16) for b in range(per)]

        top = layers - 1
        saved = []
        h = tokens
        for layer in range(top):
            u, a = up(h, w_one[layer])
            saved.append((h, u, a))
            h = (h.astype(jnp.float32) + jnp.dot(a, w_two[layer], preferred_element_type=jnp.float32)).astype(jnp.bfloat16)

        own = {}
        g = dy_loc.reshape(-1, model).astype(jnp.float32)
        gb = g.astype(jnp.bfloat16)
        who = (1 - core, core)
        u_a = [up(h, cut_top(w_one, w, 2)) for w in who]
        got = swap_cores(grad_two(u_a[0][1], gb).astype(jnp.bfloat16))
        send_a = (grad_two(u_a[1][1], gb) + got.astype(jnp.float32)).astype(jnp.bfloat16)
        gb, send_a = lax.optimization_barrier((gb, send_a))
        du = [grad_pre(gb, cut_top(w_two, w, 1), u) for w, (u, _) in zip(who, u_a)]
        own["one", top] = own_blocks(lambda v: grad_one(h, v), *du)
        for w, d in zip(who, du):
            g = g + grad_in(d, cut_top(w_one, w, 2))

        for layer in reversed(range(top)):
            h, u, a = saved[layer]
            gb = g.astype(jnp.bfloat16)
            own["two", layer] = own_blocks(lambda v: grad_two(v, gb), *(cut(a, w) for w in who))
            du = grad_pre(gb, w_two[layer], u)
            own["one", layer] = own_blocks(lambda v: grad_one(h, v), *(cut(du, w) for w in who))
            if layer > 0:
                g = g + grad_in(du, w_one[layer])
        g = g + grad_in(du, w_one[0])
        dx = g.astype(jnp.bfloat16).reshape(x_loc.shape)

        order = [("two", top)]
        for layer in reversed(range(layers)):
            order += [("one", layer)]
        order += [("two", layer) for layer in reversed(range(top))]
        names = [(k, b) for k in order for b in range(per)]
        blocks = [own[k][b] for k, b in names[per:]]
        stages = (names[:per], names[per:-1], names[-1:])
        red_a = lax.psum(send_a, "replica")
        send_b, red_a = lax.optimization_barrier((jnp.concatenate(blocks[:-1], 0), red_a))
        red_b = lax.psum(send_b, "replica")

        outs = {"one": jnp.full(w_one.shape, red_a[0, 0]), "two": jnp.full(w_two.shape, red_a[0, 0])}

        def place(red, stage):
            got = swap_cores(red)
            for src, w in ((red, core), (got, 1 - core)):
                for i, ((kind, layer), b) in enumerate(stage):
                    piece = src[i * model:(i + 1) * model][None]
                    at = (w * per + b) * model
                    start = (layer, 0, at) if kind == "one" else (layer, at, 0)
                    outs[kind] = lax.dynamic_update_slice(outs[kind], piece, start)

        place(red_a, stages[0])
        last, red_b, outs["one"], outs["two"], dx = lax.optimization_barrier((blocks[-1], red_b, outs["one"], outs["two"], dx))
        red_c = lax.psum(last, "replica")
        place(red_b, stages[1])
        red_c, outs["one"], outs["two"] = lax.optimization_barrier((red_c, outs["one"], outs["two"]))
        place(red_c, stages[2])
        return outs["one"], outs["two"], dx

    return jax.shard_map(per_device, mesh=mesh, in_specs=(P(), P(), batch_spec, batch_spec), out_specs=(P(), P(), batch_spec), check_vma=False)
```

time: 3540 us -> 1860 us (0.53)
  matrix products: 1070 us -> 440 us
  waiting for transfers between devices: 1690 us -> 1190 us
  local copies, waits for them, and re-layouts: 625 us -> 204 us
  other arithmetic: 118 us -> 0.01 us
    dot_general x51 -> x36, matrix products: 1070 us -> 440 us  [the longest x12 102 us: grad_one(): return jnp.einsum('tm,tf->mf', h, du, preferred_element_type=jnp.float32)]
    unnamed x124 -> x46, local copies, waits for them, and re-layouts: 561 us -> 0.1 us
    psum x1 -> x3, waiting for transfers between devices: 1510 us -> 1120 us  [the longest x1 1000 us: per_device(): red_b = lax.psum(send_b, 'replica')]
    all_gather x2 -> x0, waiting for transfers between devices: 179 us -> none  [reduce_grads(): return lax.all_gather(grad_shard, 'data', axis=1, tiled=True)]
    dynamic_update_slice x0 -> x18, local copies, waits for them, and re-layouts: none -> 144 us  [place(): outs[kind] = lax.dynamic_update_slice(outs[kind], piece, start)]
    another operation x3 -> x0, other arithmetic: 118 us -> none  [the longest x2 117 us: reduce_grads(): jnp.stack([part_acc.astype(jnp.bfloat16) for part_acc in accumulators])]
    ppermute x0 -> x14, waiting for transfers between devices: none -> 63.9 us  [swap_cores(): return lax.ppermute(value, 'data', SWAP)]
    psum x1 -> x0, local copies, waits for them, and re-layouts: 60.1 us -> none  [reduce_grads(): grad_shard = lax.psum(grad_shard, 'replica')]
  transfers between devices with their start and end apart: 5 -> 17, of which waited for: 3 -> 6; matrix products, arithmetic and copies ran while one was open for 18% -> 24% of each run, Pallas kernels for 0% -> 0%
where the time goes in v1:
time: 1860 us; the launch traced here: 1850 us
  waiting for transfers between devices  1190 us (64%)
  matrix products  440 us (24%)
  local copies, waits for them, and re-layouts  204 us (11%)
    psum x1, waiting for transfers between devices, per_device(): red_b = lax.psum(send_b, 'replica')  1000 us
    dynamic_update_slice x18, local copies, waits for them, and re-layouts, place(): outs[kind] = lax.dynamic_update_slice(outs[kind], piece, start)  144 us
    psum x1, waiting for transfers between devices, per_device(): red_a = lax.psum(send_a, 'replica')  118 us
    dot_general x12, matrix products, grad_one(): return jnp.einsum('tm,tf->mf', h, du, preferred_element_type=jnp.float32)  102 us
    dot_general x10, matrix products, grad_two(): return jnp.einsum('tf,tm->fm', a, gb, preferred_element_type=jnp.float32)  92.5 us
    dot_general x4, matrix products, grad_pre(): d_act = jnp.einsum('tm,fm->tf', gb, w, preferred_element_type=jnp.float32)  75.1 us
    dot_general x4, matrix products, grad_in(): return jnp.einsum('tf,mf->tm', du, w, preferred_element_type=jnp.float32)  70.7 us
    ppermute x14, waiting for transfers between devices, swap_cores(): return lax.ppermute(value, 'data', SWAP)  63.9 us
  transfers between devices with their start and end apart: 17, of which 6 were waited for; matrix products, arithmetic and copies ran while one was open for 24% of the time, Pallas kernels for 0%

profile of v1, /device:TPU:0, one launch (start us, length us, event | category | flops | bytes accessed | tf_op | source)
XLA Modules:
  0.0 1847.6 jit_solution(9101309185307665561)
XLA Ops:
  7.2 19.9 %fusion.55 = (bf16[384,7680]{1,0:T(8,128)(2,1)}, bf16[384,7680]{1,0:T(8,128)(2,1)S(1)}) fusion(bf16[384,1920]{1,0:T(8,128)(2,1)} %bitcast.199, bf16[3,1920,7680]{2,1,0:T(8,128)(2,1)} %param.4), kind=kOutput, calls=%fused_computation.77 | convolution fusion | flops 11357061120 | bytes 42762240 | tf_op jit(solution)/shard_map/dot_general | solution.py:36
  27.1 19.4 %add_convert_fusion.11 = bf16[384,1920]{1,0:T(8,128)(2,1)S(1)} fusion(bf16[384,1920]{1,0:T(8,128)(2,1)S(1)} %bitcast.200, bf16[3,7680,1920]{2,1,0:T(8,128)(2,1)} %param.5, bf16[384,7680]{1,0:T(8,128)(2,1)S(1)} %get-tuple-element.44), kind=kOutput, calls=%fused_computation.188 | convolution fusion | flops 11356323840 | bytes 38338560 | tf_op jit(solution)/shard_map/dot_general | solution.py:65
  46.6 21.0 %fusion.61 = (bf16[384,7680]{1,0:T(8,128)(2,1)}, bf16[384,7680]{1,0:T(8,128)(2,1)}) fusion(bf16[384,1920]{1,0:T(8,128)(2,1)S(1)} %add_convert_fusion.11, bf16[3,1920,7680]{2,1,0:T(8,128)(2,1)} %param.4), kind=kOutput, calls=%fused_computation.83 | convolution fusion | flops 11357061120 | bytes 42762240 | tf_op jit(solution)/shard_map/dot_general | solution.py:36
  67.6 18.4 add_convert_fusion.10
  86.0 10.9 fusion.119
  96.9 11.5 convolution_convert_fusion
  108.3 0.8 collective-permute-start
  109.2 9.9 fusion.116
  119.1 12.3 collective-permute-done
  131.4 15.3 add_convert_fusion
  146.7 12.8 fusion.100
  159.5 13.3 fusion.103
  172.9 6.3 convolution_convert_fusion.9
  179.2 6.3 convolution_convert_fusion.8
  185.5 11.4 fusion.32
  197.4 17.3 fusion.232
  214.8 24.4 %fusion.48 = bf16[384,7680]{1,0:T(8,128)(2,1)} fusion(bf16[384,7680]{1,0:T(8,128)(2,1)} %get-tuple-element.46, bf16[384,1920]{1,0:T(8,128)(2,1)} %get-tuple-element.39, bf16[3,7680,1920]{2,1,0:T(8,128)(2,1)} %param.5), kind=kOutput, calls=%fused_computation.70 | convolution fusion | flops 11386552320 | bytes 42762240 | tf_op jit(solution)/shard_map/tm,fm->tf/dot_general | solution.py:46
  239.2 7.5 convolution_convert_fusion.7
  247.1 7.9 convolution_convert_fusion.6
  255.0 21.0 %fusion.233 = (bf16[384,1920]{1,0:T(8,128)(2,1)}, f32[384,1920]{1,0:T(8,128)}) fusion(f32[384,1920]{1,0:T(8,128)S(1)} %copy-done.15, bf16[384,7680]{1,0:T(8,128)(2,1)} %fusion.48, bf16[3,1920,7680]{2,1,0:T(8,128)(2,1)} %param.4), kind=kOutput, calls=%fused_computation.255 | convolution fusion | flops 11326095360 | bytes 42762240 | tf_op jit(solution)/shard_map/tf,mf->tm/dot_general | solution.py:50
  276.1 24.5 %fusion.51 = bf16[384,7680]{1,0:T(8,128)(2,1)} fusion(bf16[384,7680]{1,0:T(8,128)(2,1)} %copy-done.16, bf16[384,1920]{1,0:T(8,128)(2,1)} %get-tuple-element.41, bf16[3,7680,1920]{2,1,0:T(8,128)(2,1)} %param.5), kind=kOutput, calls=%fused_computation.73 | convolution fusion | flops 11386552320 | bytes 42762240 | tf_op jit(solution)/shard_map/tm,fm->tf/dot_general | solution.py:46
  300.6 7.6 fusion.96
  308.7 7.9 fusion.97
  316.7 6.4 convolution_convert_fusion.3
  323.5 6.5 convolution_convert_fusion.2
  330.1 7.7 convolution_convert_fusion.1
  338.2 11.8 fusion.74
  350.0 9.1 fusion.75
  359.1 9.7 fusion.76
  368.8 9.9 fusion.77
  378.7 9.1 fusion.72
  387.8 9.1 fusion.73
  397.0 9.0 fusion.78
  406.0 9.2 fusion.79
  415.2 9.7 fusion.80
  424.8 117.5 %all-reduce.4.cloned.1.call-done = bf16[3840,1920]{1,0:T(8,128)(2,1)} async-done(((bf16[3840,1920]{1,0:T(8,128)(2,1)}), bf16[3840,1920]{1,0:T(8,128)(2,1)}) %all-reduce.4.cloned.1.call-update) | async-done | bytes 14745616 | tf_op jit(solution)/shard_map/psum | solution.py:98
  542.5 8.3 convolution_convert_fusion.10
  551.2 20.9 %add_convert_fusion.9 = bf16[384,1920]{1,0:T(8,128)(2,1)} fusion(f32[384,1920]{1,0:T(8,128)} %get-tuple-element.42, bf16[384,7680]{1,0:T(8,128)(2,1)} %fusion.51, bf16[3,1920,7680]{2,1,0:T(8,128)(2,1)} %param.4), kind=kOutput, calls=%fused_computation.177 | convolution fusion | flops 11326095360 | bytes 39813120 | tf_op jit(solution)/shard_map/tf,mf->tm/dot_general | solution.py:50
  572.1 3.5 collective-permute-done.1
  575.6 9.0 add_convert_fusion.8
  584.6 1.2 slice.170
  585.8 30.0 %broadcast_in_dim.79 = bf16[3,7680,1920]{2,1,0:T(8,128)(2,1)} broadcast(bf16[]{:T(256)} %bitcast.14), dimensions={} | broadcast | bytes 88473600 | tf_op jit(solution)/shard_map/broadcast_in_dim | solution.py:102
  615.9 7.2 bitcast_dynamic-update-slice_fusion.12
  623.0 6.7 bitcast_dynamic-update-slice_fusion.11
  629.7 6.7 fusion.91
  636.4 7.2 fusion.90
  643.6 1004.3 %all-reduce.6.cloned.1.call-done = bf16[17280,1920]{1,0:T(8,128)(2,1)} async-done(((bf16[17280,1920]{1,0:T(8,128)(2,1)}), bf16[17280,1920]{1,0:T(8,128)(2,1)}) %all-reduce.6.cloned.1.call-update) | async-done | bytes 66355216 | tf_op jit(solution)/shard_map/psum | solution.py:100
  1647.8 28.2 %broadcast_in_dim.78 = bf16[3,1920,7680]{2,1,0:T(8,128)(2,1)} broadcast(bf16[]{:T(256)} %bitcast.14), dimensions={} | broadcast | bytes 88473600 | tf_op jit(solution)/shard_map/broadcast_in_dim | solution.py:102
  1676.1 7.3 bitcast_dynamic-update-slice_fusion.10
  1683.4 6.7 bitcast_dynamic-update-slice_fusion.9
  1690.0 6.9 bitcast_dynamic-update-slice_fusion.8
  1696.9 10.8 bitcast_dynamic-update-slice_fusion.4
  1707.7 10.5 bitcast_dynamic-update-slice_fusion.3
  1718.2 11.2 bitcast_dynamic-update-slice_fusion.2
  1729.4 43.0 %collective-permute-done.12 = bf16[17280,1920]{1,0:T(8,128)(2,1)} collective-permute-done((bf16[17280,1920]{1,0:T(8,128)(2,1)}, bf16[17280,1920]{1,0:T(8,128)(2,1)}, u32[]{:S(2)}, u32[]{:S(2)}) %collective-permute-start.12) | collective-permute-done | bytes 66355232 | tf_op jit(solution)/shard_map/ppermute | solution.py:15
  1772.4 6.7 fusion.89
  1779.1 7.6 fusion.88
  1786.7 6.7 fusion.87
  1793.4 10.8 fusion.83
  1804.1 10.7 fusion.82
  1814.8 10.5 fusion.81
  1825.5 6.7 bitcast_dynamic-update-slice_fusion.1
  1832.1 5.1 collective-permute-done.13
  1837.2 3.6 bitcast_dynamic-update-slice_fusion
  (79 shorter events, 3.3 us)
Async XLA Ops:
  7.2 535.2 %all-reduce.4.cloned.1.call-start = ((), (), s32[]{:S(2)}) async-start(), calls=%async_computation | async-start | bytes 29491200 | tf_op jit(solution)/shard_map/psum | solution.py:98
  7.2 19.9 %copy-start.1 = (bf16[3,2,64,1920]{3,2,1,0:T(8,128)(2,1)S(1)}, bf16[3,2,64,1920]{3,2,1,0:T(8,128)(2,1)}, u32[]{:S(2)}) copy-start(bf16[3,2,64,1920]{3,2,1,0:T(8,128)(2,1)} %param.6) | copy-start | bytes 4423684
  27.1 19.4 %copy-start.16 = (bf16[384,7680]{1,0:T(8,128)(2,1)}, bf16[384,7680]{1,0:T(8,128)(2,1)S(1)}, u32[]{:S(2)}) copy-start(bf16[384,7680]{1,0:T(8,128)(2,1)S(1)} %get-tuple-element.44) | copy-start | bytes 17694724
  46.5 21.0 %copy-start.3 = (bf16[384,1920]{1,0:T(8,128)(2,1)}, bf16[384,1920]{1,0:T(8,128)(2,1)S(1)}, u32[]{:S(2)}) copy-start(bf16[384,1920]{1,0:T(8,128)(2,1)S(1)} %add_convert_fusion.11) | copy-start | bytes 4423684
  86.0 93.2 %copy-start.5 = (bf16[384,1920]{1,0:T(8,128)(2,1)}, bf16[384,1920]{1,0:T(8,128)(2,1)S(1)}, u32[]{:S(2)}) copy-start(bf16[384,1920]{1,0:T(8,128)(2,1)S(1)} %add_convert_fusion.10) | copy-start | bytes 4423684
  86.0 10.9 copy-start
  96.8 11.5 copy-start.14
  108.3 23.0 %collective-permute-start = (bf16[3840,1920]{1,0:T(8,128)(2,1)}, bf16[3840,1920]{1,0:T(8,128)(2,1)}, u32[]{:S(2)}, u32[]{:S(2)}) collective-permute-start(bf16[3840,1920]{1,0:T(8,128)(2,1)} %convolution_convert_fusion), channel_id=1, source_target_pairs={{0,1},{1,0},{2,3},{3,2},{4,5},{5,4},{6,7},{7,6}} | collective-permute-start | bytes 44236808 | tf_op jit(solution)/shard_map/ppermute | solution.py:15
  119.1 12.3 copy-start.12
  146.7 12.8 copy-start.13
  196.9 119.7 %collective-permute-start.2 = (bf16[1920,1920]{1,0:T(8,128)(2,1)}, bf16[1920,1920]{1,0:T(8,128)(2,1)}, u32[]{:S(2)}, u32[]{:S(2)}) collective-permute-start(bf16[1920,1920]{1,0:T(8,128)(2,1)} %convolution_convert_fusion.9), channel_id=1, source_target_pairs={{0,1},{1,0},{2,3},{3,2},{4,5},{5,4},{6,7},{7,6}} | collective-permute-start | bytes 22118408 | tf_op jit(solution)/shard_map/ppermute | solution.py:15
  197.3 125.8 %collective-permute-start.3 = (bf16[1920,1920]{1,0:T(8,128)(2,1)}, bf16[1920,1920]{1,0:T(8,128)(2,1)}, u32[]{:S(2)}, u32[]{:S(2)}) collective-permute-start(bf16[1920,1920]{1,0:T(8,128)(2,1)} %convolution_convert_fusion.8), channel_id=1, source_target_pairs={{0,1},{1,0},{2,3},{3,2},{4,5},{5,4},{6,7},{7,6}} | collective-permute-start | bytes 22118408 | tf_op jit(solution)/shard_map/ppermute | solution.py:15
  214.7 24.4 %copy-start.4 = (bf16[384,1920]{1,0:T(8,128)(2,1)S(1)}, bf16[384,1920]{1,0:T(8,128)(2,1)}, u32[]{:S(2)}) copy-start(bf16[384,1920]{1,0:T(8,128)(2,1)} %copy-done.3) | copy-start | bytes 4423684
  246.7 8.3 copy-start.15
  246.7 83.3 %collective-permute-start.4 = (bf16[1920,1920]{1,0:T(8,128)(2,1)}, bf16[1920,1920]{1,0:T(8,128)(2,1)}, u32[]{:S(2)}, u32[]{:S(2)}) collective-permute-start(bf16[1920,1920]{1,0:T(8,128)(2,1)} %convolution_convert_fusion.7), channel_id=1, source_target_pairs={{0,1},{1,0},{2,3},{3,2},{4,5},{5,4},{6,7},{7,6}} | collective-permute-start | bytes 22118408 | tf_op jit(solution)/shard_map/ppermute | solution.py:15
  255.0 82.9 %collective-permute-start.5 = (bf16[1920,1920]{1,0:T(8,128)(2,1)}, bf16[1920,1920]{1,0:T(8,128)(2,1)}, u32[]{:S(2)}, u32[]{:S(2)}) collective-permute-start(bf16[1920,1920]{1,0:T(8,128)(2,1)} %convolution_convert_fusion.6), channel_id=1, source_target_pairs={{0,1},{1,0},{2,3},{3,2},{4,5},{5,4},{6,7},{7,6}} | collective-permute-start | bytes 22118408 | tf_op jit(solution)/shard_map/ppermute | solution.py:15
  276.0 1371.8 %all-reduce.6.cloned.1.call-start = ((), (), s32[]{:S(2)}) async-start(), calls=%async_computation.1 | async-start | bytes 132710400 | tf_op jit(solution)/shard_map/psum | solution.py:100
  276.1 24.5 %copy-start.2 = (bf16[3,2,64,1920]{3,2,1,0:T(8,128)(2,1)S(1)}, bf16[3,2,64,1920]{3,2,1,0:T(8,128)(2,1)}, u32[]{:S(2)}) copy-start(bf16[3,2,64,1920]{3,2,1,0:T(8,128)(2,1)} %param.6) | copy-start | bytes 4423684
  300.6 16.1 slice-start
  308.2 8.5 slice-start.1
  308.2 8.5 copy-start.9
  308.2 70.5 %collective-permute-start.6 = (bf16[1920,1920]{1,0:T(8,128)(2,1)}, bf16[1920,1920]{1,0:T(8,128)(2,1)}, u32[]{:S(2)}, u32[]{:S(2)}) collective-permute-start(bf16[1920,1920]{1,0:T(8,128)(2,1)} %fusion.96), channel_id=1, source_target_pairs={{0,1},{1,0},{2,3},{3,2},{4,5},{5,4},{6,7},{7,6}} | collective-permute-start | bytes 22118408 | tf_op jit(solution)/shard_map/ppermute | solution.py:15
  316.6 71.2 %collective-permute-start.7 = (bf16[1920,1920]{1,0:T(8,128)(2,1)}, bf16[1920,1920]{1,0:T(8,128)(2,1)}, u32[]{:S(2)}, u32[]{:S(2)}) collective-permute-start(bf16[1920,1920]{1,0:T(8,128)(2,1)} %fusion.97), channel_id=1, source_target_pairs={{0,1},{1,0},{2,3},{3,2},{4,5},{5,4},{6,7},{7,6}} | collective-permute-start | bytes 22118408 | tf_op jit(solution)/shard_map/ppermute | solution.py:15
  323.1 7.1 copy-start.7
  323.1 73.9 %collective-permute-start.8 = (bf16[1920,1920]{1,0:T(8,128)(2,1)}, bf16[1920,1920]{1,0:T(8,128)(2,1)}, u32[]{:S(2)}, u32[]{:S(2)}) collective-permute-start(bf16[1920,1920]{1,0:T(8,128)(2,1)} %convolution_convert_fusion.3), channel_id=1, source_target_pairs={{0,1},{1,0},{2,3},{3,2},{4,5},{5,4},{6,7},{7,6}} | collective-permute-start | bytes 22118408 | tf_op jit(solution)/shard_map/ppermute | solution.py:15
  330.0 76.0 %collective-permute-start.9 = (bf16[1920,1920]{1,0:T(8,128)(2,1)}, bf16[1920,1920]{1,0:T(8,128)(2,1)}, u32[]{:S(2)}, u32[]{:S(2)}) collective-permute-start(bf16[1920,1920]{1,0:T(8,128)(2,1)} %convolution_convert_fusion.2), channel_id=1, source_target_pairs={{0,1},{1,0},{2,3},{3,2},{4,5},{5,4},{6,7},{7,6}} | collective-permute-start | bytes 22118408 | tf_op jit(solution)/shard_map/ppermute | solution.py:15
  337.8 77.3 %collective-permute-start.10 = (bf16[1920,1920]{1,0:T(8,128)(2,1)}, bf16[1920,1920]{1,0:T(8,128)(2,1)}, u32[]{:S(2)}, u32[]{:S(2)}) collective-permute-start(bf16[1920,1920]{1,0:T(8,128)(2,1)} %convolution_convert_fusion.1), channel_id=1, source_target_pairs={{0,1},{1,0},{2,3},{3,2},{4,5},{5,4},{6,7},{7,6}} | collective-permute-start | bytes 22118408 | tf_op jit(solution)/shard_map/ppermute | solution.py:15
  338.2 11.8 copy-start.6
  338.2 11.8 copy-start.11
  359.1 19.6 %slice-start.4 = ((s8[5898240]{0:T(1024)(128)(4,1)}), s8[4194304]{0:T(1024)(128)(4,1)S(1)}, s32[]{:S(2)}) async-start(s8[5898240]{0:T(1024)(128)(4,1)} %bitcast.210), calls=%async_computation.7 | async-start | bytes 8388608
  368.8 9.9 slice-start.5
  378.7 18.2 slice-start.2
  387.8 9.1 slice-start.3
  387.8 9.1 copy-start.10
  406.0 9.2 copy-start.8
  542.4 1282.9 %all-reduce.8.cloned.1.call-start = ((), (), s32[]{:S(2)}) async-start(), calls=%async_computation.2 | async-start | bytes 14745600 | tf_op jit(solution)/shard_map/psum | solution.py:115
  542.4 87.3 %collective-permute-start.11 = (bf16[3840,1920]{1,0:T(8,128)(2,1)}, bf16[3840,1920]{1,0:T(8,128)(2,1)}, u32[]{:S(2)}, u32[]{:S(2)}) collective-permute-start(bf16[3840,1920]{1,0:T(8,128)(2,1)} %all-reduce.4.cloned.1.call-done), channel_id=1, source_target_pairs={{0,1},{1,0},{2,3},{3,2},{4,5},{5,4},{6,7},{7,6}} | collective-permute-start | bytes 44236808 | tf_op jit(solution)/shard_map/ppermute | solution.py:15
  550.7 24.9 %collective-permute-start.1 = (bf16[1920,1920]{1,0:T(8,128)(2,1)}, bf16[1920,1920]{1,0:T(8,128)(2,1)}, u32[]{:S(2)}, u32[]{:S(2)}) collective-permute-start(bf16[1920,1920]{1,0:T(8,128)(2,1)} %convolution_convert_fusion.10), channel_id=1, source_target_pairs={{0,1},{1,0},{2,3},{3,2},{4,5},{5,4},{6,7},{7,6}} | collective-permute-start | bytes 22118408 | tf_op jit(solution)/shard_map/ppermute | solution.py:15
  1676.0 96.4 %collective-permute-start.12 = (bf16[17280,1920]{1,0:T(8,128)(2,1)}, bf16[17280,1920]{1,0:T(8,128)(2,1)}, u32[]{:S(2)}, u32[]{:S(2)}) collective-permute-start(bf16[17280,1920]{1,0:T(8,128)(2,1)} %all-reduce.6.cloned.1.call-done), channel_id=1, source_target_pairs={{0,1},{1,0},{2,3},{3,2},{4,5},{5,4},{6,7},{7,6}} | collective-permute-start | bytes 199065600 | tf_op jit(solution)/shard_map/ppermute | solution.py:15
  1825.3 11.9 collective-permute-start.13
Sparse Core Ops, SparseCore 0:
  276.2 266.1 all-reduce.3
  546.4 1101.3 all-reduce.5
  1676.2 147.4 all-reduce.7

commit v2 on v0

v2 whole, which is shorter than its diff:
```python
import jax
import jax.numpy as jnp
from jax import lax
from jax.sharding import PartitionSpec as P


BOTH = ("replica", "data")


def hop(axes):
    return [(2 * r + c, 2 * (r ^ (1 << axes[c])) + c) for r in range(4) for c in range(2)]


FIRST, SECOND = hop((0, 1)), hop((1, 0))


def gelu_tanh(value):
    return jax.nn.gelu(value, approximate=True)


def add_up(*terms):
    return sum(t.astype(jnp.float32) for t in terms).astype(jnp.bfloat16)


def solution(mesh):
    batch_spec = P(("replica", "data"))

    def per_device(w_one, w_two, x_loc, dy_loc):
        layers, model, hidden = w_one.shape
        size = hidden // 4
        rows = model // 2
        top = layers - 1
        chip, core = lax.axis_index("replica"), lax.axis_index("data")
        pos_x, pos_y = chip % 2, chip // 2
        f = jnp.where(core == 0, pos_x, pos_y)
        s = jnp.where(core == 0, pos_y, pos_x)
        away_send, away_keep = (1 - core) * 2 + 1 - s, (1 - core) * 2 + s
        own_send, own_keep = core * 2 + 1 - f, core * 2 + f

        def swap(value):
            return lax.ppermute(value, "data", [(0, 1), (1, 0)])

        def first(value):
            return lax.ppermute(value, BOTH, FIRST)

        def second(value):
            return lax.ppermute(value, BOTH, SECOND)

        def grad_one(h, du):
            return jnp.einsum("tm,tf->mf", h, du, preferred_element_type=jnp.float32)

        def grad_two(a, gb):
            return jnp.einsum("tf,tm->fm", a, gb, preferred_element_type=jnp.float32)

        def grad_pre(gb, w, u):
            d_act = jnp.einsum("tm,fm->tf", gb, w, preferred_element_type=jnp.float32)
            return jax.vjp(gelu_tanh, u.astype(jnp.float32))[1](d_act)[0].astype(jnp.bfloat16)

        def grad_in(du, w):
            return jnp.einsum("tf,mf->tm", du, w, preferred_element_type=jnp.float32)

        def up(h, w):
            u = jnp.dot(h, w, preferred_element_type=jnp.float32).astype(jnp.bfloat16)
            return u, gelu_tanh(u.astype(jnp.float32)).astype(jnp.bfloat16)

        def cut_top(w, block, axis):
            start, shape = [top, 0, 0], [1, *w.shape[1:]]
            start[axis], shape[axis] = block * size, size
            return lax.dynamic_slice(w, start, shape)[0]

        def cut(wide):
            return lambda block: lax.dynamic_slice_in_dim(wide, block * size, size, 1)

        def chip_sum(dot, away, own):
            return add_up(dot(own), swap(dot(away).astype(jnp.bfloat16)))

        def half(value, which):
            return lax.dynamic_slice_in_dim(value, which * rows, rows, 0)

        def for_second(got_first, keep):
            return add_up(half(keep, 1 - s), half(got_first, 1 - s))

        def summed(got_first, keep, got_second):
            return add_up(half(keep, s), half(got_first, s), got_second)

        saved = []
        h = x_loc.reshape(-1, model)
        for layer in range(top):
            u, a = up(h, w_one[layer])
            saved.append((h, u, a))
            h = (h.astype(jnp.float32) + jnp.dot(a, w_two[layer], preferred_element_type=jnp.float32)).astype(jnp.bfloat16)

        g = dy_loc.reshape(-1, model).astype(jnp.float32)
        gb = g.astype(jnp.bfloat16)
        where = {"away_send": away_send, "own_send": own_send, "away_keep": away_keep, "own_keep": own_keep}

        def top_two(kind, h, gb):
            pairs = [up(h, cut_top(w_one, where[side + kind], 2)) for side in ("away_", "own_")]
            got = swap(grad_two(pairs[0][1], gb).astype(jnp.bfloat16))
            return [u for u, _ in pairs], add_up(grad_two(pairs[1][1], gb), got)

        def top_one(kind, h, gb, u):
            du = [grad_pre(gb, cut_top(w_two, where[side + kind], 1), v) for side, v in zip(("away_", "own_"), u)]
            got = swap(grad_one(h, du[0]).astype(jnp.bfloat16))
            return du, add_up(grad_one(h, du[1]), got)

        gate = lax.optimization_barrier
        u_send, two_send = top_two("send", h, gb)
        two_got = first(two_send)
        gb_one, two_send = gate((gb, two_send))
        du_send, one_send = top_one("send", h, gb_one, u_send)
        one_got = first(one_send)
        h_keep, gb_keep, one_send = gate((h, gb_one, one_send))
        u_keep, two_keep = top_two("keep", h_keep, gb_keep)
        du_keep, one_keep = top_one("keep", h_keep, gb_keep, u_keep)
        two_on = for_second(two_got, two_keep)
        two_got_second = second(two_on)
        du_send, du_keep, two_on, one_keep = gate((du_send, du_keep, two_on, one_keep))
        for kind, du in (("send", du_send), ("keep", du_keep)):
            for side, d in zip(("away_", "own_"), du):
                g = g + grad_in(d, cut_top(w_one, where[side + kind], 2))
        h, u, a = saved[1]
        gb = g.astype(jnp.bfloat16)
        part = cut(a)
        mid_send = chip_sum(lambda v: grad_two(v, gb), part(away_send), part(own_send))
        one_on = for_second(one_got, one_keep)
        mid_got = first(mid_send)
        one_got_second = second(one_on)
        gb_pre, mid_send, one_on = gate((gb, mid_send, one_on))
        du = grad_pre(gb_pre, w_two[1], u)
        two_sum = summed(two_got, two_keep, two_got_second)
        two_pieces = [(two_sum, f, s), (second(two_sum), f, 1 - s), (first(two_sum), 1 - f, s)]
        du, two_sum = gate((du, two_sum))
        part_one = cut(du)
        low_send = chip_sum(lambda v: grad_one(h, v), part_one(away_send), part_one(own_send))
        mid_keep = chip_sum(lambda v: grad_two(v, gb), part(away_keep), part(own_keep))
        low_keep = chip_sum(lambda v: grad_one(h, v), part_one(away_keep), part_one(own_keep))
        low_got = first(low_send)
        du, low_send, mid_keep, low_keep = gate((du, low_send, mid_keep, low_keep))
        g = g + grad_in(du, w_one[1])
        h, u, a = saved[0]
        gb = g.astype(jnp.bfloat16)
        du = grad_pre(gb, w_two[0], u)
        last = []
        for wide, dot in ((a, lambda v: grad_two(v, gb)), (du, lambda v: grad_one(h, v))):
            part = cut(wide)
            got = first(chip_sum(dot, part(away_send), part(own_send)))
            last.append((got, chip_sum(dot, part(away_keep), part(own_keep))))
        g = g + grad_in(du, w_one[0])
        dx = g.astype(jnp.bfloat16).reshape(x_loc.shape)

        outs = {"one": jnp.full(w_one.shape, two_got[0, 0]), "two": jnp.full(w_two.shape, two_got[0, 0])}
        units = [
            ("two", 2, two_got, two_keep, two_got_second),
            ("one", 2, one_got, one_keep, one_got_second),
            ("two", 1, mid_got, mid_keep, None),
            ("one", 1, low_got, low_keep, None),
            ("two", 0, *last[0], None),
            ("one", 0, *last[1], None),
        ]
        for kind, layer, got_first, keep, got_second in units:
            if got_second is None:
                got_second = second(for_second(got_first, keep))
            if (kind, layer) == ("two", 2):
                pieces = two_pieces
            else:
                done = summed(got_first, keep, got_second)
                pieces = [(done, f, s), (second(done), f, 1 - s), (first(done), 1 - f, s)]
            pieces = pieces + [(first(pieces[1][0]), 1 - f, 1 - s)]

            def put(value, block, row):
                at = (layer, row * rows, block * size) if kind == "one" else (layer, block * size + row * rows, 0)
                outs[kind] = lax.dynamic_update_slice(outs[kind], value[None], at)

            for value, block, row in pieces:
                put(value, core * 2 + block, row)
            for (value, _, _), (block, row) in zip(pieces, ((s, f), (s, 1 - f), (1 - s, f), (1 - s, 1 - f))):
                put(swap(value), (1 - core) * 2 + block, row)
        return outs["one"], outs["two"], dx

    return jax.shard_map(per_device, mesh=mesh, in_specs=(P(), P(), batch_spec, batch_spec), out_specs=(P(), P(), batch_spec), check_vma=False)
```

time: 3540 us -> 1650 us (0.47)
  waiting for transfers between devices: 1690 us -> 842 us
  matrix products: 1070 us -> 460 us
  local copies, waits for them, and re-layouts: 625 us -> 212 us
  starting transfers between devices: 0.2 us -> 55.8 us
  other arithmetic: 118 us -> 68.6 us
    psum x1 -> x0, waiting for transfers between devices: 1510 us -> none  [reduce_grads(): grad_shard = lax.psum(grad_shard, 'replica')]
    ppermute x0 -> x66, waiting for transfers between devices: none -> 842 us  [the longest x18 645 us: first(): return lax.ppermute(value, BOTH, FIRST)]
    dot_general x51 -> x44, matrix products: 1070 us -> 460 us  [the longest x12 100 us: grad_two(): return jnp.einsum('tf,tm->fm', a, gb, preferred_element_type=jnp.float32)]
    unnamed x124 -> x74, local copies, waits for them, and re-layouts: 561 us -> 0.16 us
    all_gather x2 -> x0, waiting for transfers between devices: 179 us -> none  [reduce_grads(): return lax.all_gather(grad_shard, 'data', axis=1, tiled=True)]
    dynamic_update_slice x0 -> x42, local copies, waits for them, and re-layouts: none -> 154 us  [put(): outs[kind] = lax.dynamic_update_slice(outs[kind], value[None], at)]
    another operation x3 -> x0, other arithmetic: 118 us -> none  [the longest x2 117 us: reduce_grads(): jnp.stack([part_acc.astype(jnp.bfloat16) for part_acc in accumulators])]
    psum x1 -> x0, local copies, waits for them, and re-layouts: 60.1 us -> none  [reduce_grads(): grad_shard = lax.psum(grad_shard, 'replica')]
  transfers between devices with their start and end apart: 5 -> 66, of which waited for: 3 -> 21; matrix products, arithmetic and copies ran while one was open for 18% -> 37% of each run, Pallas kernels for 0% -> 0%
where the time goes in v2:
time: 1650 us; the launch traced here: 1640 us
  waiting for transfers between devices  842 us (51%)
  matrix products  460 us (28%)
  local copies, waits for them, and re-layouts  212 us (13%)
  other arithmetic  68.6 us (4%)
  starting transfers between devices  55.8 us (3%)
    ppermute x18, waiting for transfers between devices, first(): return lax.ppermute(value, BOTH, FIRST)  645 us
    ppermute x12, waiting for transfers between devices, second(): return lax.ppermute(value, BOTH, SECOND)  189 us
    dynamic_update_slice x42, local copies, waits for them, and re-layouts, put(): outs[kind] = lax.dynamic_update_slice(outs[kind], value[None], at)  154 us
    dot_general x12, matrix products, grad_two(): return jnp.einsum('tf,tm->fm', a, gb, preferred_element_type=jnp.float32)  100 us
    dot_general x12, matrix products, grad_one(): return jnp.einsum('tm,tf->mf', h, du, preferred_element_type=jnp.float32)  96.2 us
    dot_general x6, matrix products, grad_pre(): d_act = jnp.einsum('tm,fm->tf', gb, w, preferred_element_type=jnp.float32)  80.5 us
    dot_general x6, matrix products, grad_in(): return jnp.einsum('tf,mf->tm', du, w, preferred_element_type=jnp.float32)  78.7 us
    dot_general x6, matrix products, up(): u = jnp.dot(h, w, preferred_element_type=jnp.float32).astype(jnp.bfloat16)  66.9 us
  transfers between devices with their start and end apart: 66, of which 21 were waited for; matrix products, arithmetic and copies ran while one was open for 37% of the time, Pallas kernels for 0%

profile of v2, /device:TPU:0, one launch (start us, length us, event | category | flops | bytes accessed | tf_op | source)
XLA Modules:
  0.0 1640.1 jit_solution(3932694178695387402)
XLA Ops:
  0.7 19.9 %fusion.37 = (bf16[384,7680]{1,0:T(8,128)(2,1)}, bf16[384,7680]{1,0:T(8,128)(2,1)S(1)}) fusion(bf16[384,1920]{1,0:T(8,128)(2,1)} %bitcast.271, bf16[3,1920,7680]{2,1,0:T(8,128)(2,1)} %param.4), kind=kOutput, calls=%fused_computation.59 | convolution fusion | flops 11357061120 | bytes 42762240 | tf_op jit(solution)/shard_map/dot_general | solution.py:63
  20.6 19.4 %add_convert_fusion.24 = bf16[384,1920]{1,0:T(8,128)(2,1)S(1)} fusion(bf16[384,1920]{1,0:T(8,128)(2,1)S(1)} %bitcast.272, bf16[3,7680,1920]{2,1,0:T(8,128)(2,1)} %param.5, bf16[384,7680]{1,0:T(8,128)(2,1)S(1)} %get-tuple-element.48), kind=kOutput, calls=%fused_computation.243 | convolution fusion | flops 11356323840 | bytes 38338560 | tf_op jit(solution)/shard_map/dot_general | solution.py:91
  40.0 21.0 %fusion.43 = (bf16[384,7680]{1,0:T(8,128)(2,1)}, bf16[384,7680]{1,0:T(8,128)(2,1)}) fusion(bf16[384,1920]{1,0:T(8,128)(2,1)S(1)} %add_convert_fusion.24, bf16[3,1920,7680]{2,1,0:T(8,128)(2,1)} %param.4), kind=kOutput, calls=%fused_computation.65 | convolution fusion | flops 11357061120 | bytes 42762240 | tf_op jit(solution)/shard_map/dot_general | solution.py:63
  61.0 18.5 %add_convert_fusion.23 = bf16[384,1920]{1,0:T(8,128)(2,1)S(1)} fusion(bf16[384,1920]{1,0:T(8,128)(2,1)S(1)} %add_convert_fusion.24, bf16[3,7680,1920]{2,1,0:T(8,128)(2,1)} %param.5, bf16[384,7680]{1,0:T(8,128)(2,1)} %get-tuple-element.44), kind=kOutput, calls=%fused_computation.242 | convolution fusion | flops 11356323840 | bytes 38338560 | tf_op jit(solution)/shard_map/dot_general | solution.py:91
  79.5 6.6 fusion.148
  86.1 6.9 convolution_convert_fusion.11
  93.9 6.5 fusion.145
  105.5 9.2 add_convert_fusion.9
  114.8 7.7 fusion.106
  129.1 8.8 fusion.109
  140.8 9.0 add_convert_fusion.8
  149.7 6.5 fusion.151
  156.2 7.3 convolution_convert_fusion.9
  164.1 7.6 fusion.103
  171.7 6.5 convolution_convert_fusion.8
  187.8 7.7 fusion.100
  195.5 9.6 add_convert_fusion.7
  205.0 6.9 add_convert_fusion.6
  211.9 50.2 %collective-permute-done.1 = bf16[1920,1920]{1,0:T(8,128)(2,1)} collective-permute-done((bf16[1920,1920]{1,0:T(8,128)(2,1)}, bf16[1920,1920]{1,0:T(8,128)(2,1)}, u32[]{:S(2)}, u32[]{:S(2)}) %collective-permute-start.1) | collective-permute-done | bytes 7372832 | tf_op jit(solution)/shard_map/ppermute | solution.py:44
  268.0 8.2 fusion.68
  276.3 8.2 fusion.72
  284.5 8.1 fusion.58
  292.6 11.3 fusion.283
  303.8 8.2 convolution_convert_fusion.7
  314.1 52.2 %collective-permute-done.5 = bf16[1920,1920]{1,0:T(8,128)(2,1)S(1)} collective-permute-done((bf16[1920,1920]{1,0:T(8,128)(2,1)}, bf16[1920,1920]{1,0:T(8,128)(2,1)S(1)}, u32[]{:S(2)}, u32[]{:S(2)}) %collective-permute-start.5) | collective-permute-done | bytes 7372832 | tf_op jit(solution)/shard_map/ppermute | solution.py:44
  371.9 7.9 convolution_convert_fusion.5
  381.0 28.3 %broadcast_in_dim.175 = bf16[3,7680,1920]{2,1,0:T(8,128)(2,1)} broadcast(bf16[]{:T(256)} %bitcast.8), dimensions={} | broadcast | bytes 88473600 | tf_op jit(solution)/shard_map/broadcast_in_dim | solution.py:152
  409.3 7.5 bitcast_dynamic-update-slice_fusion.23
  419.9 28.2 %broadcast_in_dim.150 = bf16[3,1920,7680]{2,1,0:T(8,128)(2,1)} broadcast(bf16[]{:T(256)} %bitcast.8), dimensions={} | broadcast | bytes 88473600 | tf_op jit(solution)/shard_map/broadcast_in_dim | solution.py:152
  448.1 7.6 bitcast_dynamic-update-slice_fusion.47
  457.8 8.9 add_convert_fusion.5
  466.7 24.2 %fusion.30 = bf16[384,7680]{1,0:T(8,128)(2,1)} fusion(bf16[384,7680]{1,0:T(8,128)(2,1)} %get-tuple-element.44, bf16[384,1920]{1,0:T(8,128)(2,1)S(1)} %copy-done.14, bf16[3,7680,1920]{2,1,0:T(8,128)(2,1)} %param.5), kind=kOutput, calls=%fused_computation.52 | convolution fusion | flops 11386552320 | bytes 42762240 | tf_op jit(solution)/shard_map/tm,fm->tf/dot_general | solution.py:56
  493.4 7.5 convolution_convert_fusion.6
  501.5 7.5 convolution_convert_fusion.4
  509.5 68.7 %collective-permute-done.8 = bf16[960,1920]{1,0:T(8,128)(2,1)} collective-permute-done((bf16[960,1920]{1,0:T(8,128)(2,1)}, bf16[960,1920]{1,0:T(8,128)(2,1)}, u32[]{:S(2)}, u32[]{:S(2)}) %collective-permute-start.8) | collective-permute-done | bytes 3686432 | tf_op jit(solution)/shard_map/ppermute | solution.py:44
  588.7 7.2 add_convert_fusion.3
  595.9 101.4 %collective-permute-done.41 = bf16[960,1920]{1,0:T(8,128)(2,1)} collective-permute-done((bf16[960,1920]{1,0:T(8,128)(2,1)}, bf16[960,1920]{1,0:T(8,128)(2,1)}, u32[]{:S(2)}, u32[]{:S(2)}) %collective-permute-start.41) | collective-permute-done | bytes 3686432 | tf_op jit(solution)/shard_map/ppermute | solution.py:44
  707.5 9.2 add_convert_fusion.4
  722.1 8.9 add_convert_fusion.2
  738.7 12.6 collective-permute-done.9
  751.8 21.8 %fusion.284 = (bf16[384,1920]{1,0:T(8,128)(2,1)}, f32[384,1920]{1,0:T(8,128)}) fusion(f32[384,1920]{1,0:T(8,128)} %get-tuple-element.42, bf16[384,7680]{1,0:T(8,128)(2,1)} %fusion.30, bf16[3,1920,7680]{2,1,0:T(8,128)(2,1)} %param.4), kind=kOutput, calls=%fused_computation.346 | convolution fusion | flops 11326095360 | bytes 42762240 | tf_op jit(solution)/shard_map/tf,mf->tm/dot_general | solution.py:60
  773.7 9.0 convolution_convert_fusion
  782.7 35.9 %collective-permute-done.47 = bf16[960,1920]{1,0:T(8,128)(2,1)S(1)} collective-permute-done((bf16[960,1920]{1,0:T(8,128)(2,1)}, bf16[960,1920]{1,0:T(8,128)(2,1)S(1)}, u32[]{:S(2)}, u32[]{:S(2)}) %collective-permute-start.47) | collective-permute-done | bytes 3686432 | tf_op jit(solution)/shard_map/ppermute | solution.py:47
  818.6 7.7 convolution_convert_fusion.1
  830.4 6.5 bitcast_dynamic-update-slice_fusion.15
  839.8 46.8 %collective-permute-done.19 = bf16[1920,1920]{1,0:T(8,128)(2,1)} collective-permute-done((bf16[1920,1920]{1,0:T(8,128)(2,1)}, bf16[1920,1920]{1,0:T(8,128)(2,1)}, u32[]{:S(2)}, u32[]{:S(2)}) %collective-permute-start.19) | collective-permute-done | bytes 7372832 | tf_op jit(solution)/shard_map/ppermute | solution.py:44
  886.6 24.5 %fusion.33 = bf16[384,7680]{1,0:T(8,128)(2,1)} fusion(bf16[384,7680]{1,0:T(8,128)(2,1)} %copy-done.24, bf16[384,1920]{1,0:T(8,128)(2,1)} %get-tuple-element.45, bf16[3,7680,1920]{2,1,0:T(8,128)(2,1)} %param.5), kind=kOutput, calls=%fused_computation.55 | convolution fusion | flops 11386552320 | bytes 42762240 | tf_op jit(solution)/shard_map/tm,fm->tf/dot_general | solution.py:56
  911.1 7.6 fusion.85
  918.7 7.6 fusion.84
  926.3 16.4 %collective-permute-done.49 = bf16[960,1920]{1,0:T(8,128)(2,1)} collective-permute-done((bf16[960,1920]{1,0:T(8,128)(2,1)}, bf16[960,1920]{1,0:T(8,128)(2,1)}, u32[]{:S(2)}, u32[]{:S(2)}) %collective-permute-start.49) | collective-permute-done | bytes 3686432 | tf_op jit(solution)/shard_map/ppermute | solution.py:44
  949.5 9.1 add_convert_fusion
  972.6 48.9 %collective-permute-done.20 = bf16[960,1920]{1,0:T(8,128)(2,1)} collective-permute-done((bf16[960,1920]{1,0:T(8,128)(2,1)}, bf16[960,1920]{1,0:T(8,128)(2,1)}, u32[]{:S(2)}, u32[]{:S(2)}) %collective-permute-start.20) | collective-permute-done | bytes 3686432 | tf_op jit(solution)/shard_map/ppermute | solution.py:47
  1048.7 9.4 fusion.26
  1058.0 90.4 %collective-permute-done.50 = bf16[960,1920]{1,0:T(8,128)(2,1)} collective-permute-done((bf16[960,1920]{1,0:T(8,128)(2,1)}, bf16[960,1920]{1,0:T(8,128)(2,1)}, u32[]{:S(2)}, u32[]{:S(2)}) %collective-permute-start.50) | collective-permute-done | bytes 3686432 | tf_op jit(solution)/shard_map/ppermute | solution.py:44
  1149.4 9.1 add_convert_fusion.1
  1164.1 9.8 fusion.27
  1192.5 114.0 %collective-permute-done.22 = bf16[960,1920]{1,0:T(8,128)(2,1)} collective-permute-done((bf16[960,1920]{1,0:T(8,128)(2,1)S(1)}, bf16[960,1920]{1,0:T(8,128)(2,1)}, u32[]{:S(2)}, u32[]{:S(2)}) %collective-permute-start.22) | collective-permute-done | bytes 3686432 | tf_op jit(solution)/shard_map/ppermute | solution.py:44
  1317.9 8.6 bitcast_dynamic-update-slice_fusion.7
  1328.1 33.9 %collective-permute-done.23 = bf16[960,1920]{1,0:T(8,128)(2,1)} collective-permute-done((bf16[960,1920]{1,0:T(8,128)(2,1)}, bf16[960,1920]{1,0:T(8,128)(2,1)}, u32[]{:S(2)}, u32[]{:S(2)}) %collective-permute-start.23) | collective-permute-done | bytes 3686432 | tf_op jit(solution)/shard_map/ppermute | solution.py:44
  1398.5 74.4 %collective-permute-done.31 = bf16[960,1920]{1,0:T(8,128)(2,1)} collective-permute-done((bf16[960,1920]{1,0:T(8,128)(2,1)S(1)}, bf16[960,1920]{1,0:T(8,128)(2,1)}, u32[]{:S(2)}, u32[]{:S(2)}) %collective-permute-start.31) | collective-permute-done | bytes 3686432 | tf_op jit(solution)/shard_map/ppermute | solution.py:47
  1483.2 21.1 %add_convert_fusion.22 = bf16[384,1920]{1,0:T(8,128)(2,1)} fusion(f32[384,1920]{1,0:T(8,128)} %get-tuple-element.46, bf16[384,7680]{1,0:T(8,128)(2,1)} %fusion.33, bf16[3,1920,7680]{2,1,0:T(8,128)(2,1)} %param.4), kind=kOutput, calls=%fused_computation.240 | convolution fusion | flops 11326095360 | bytes 39813120 | tf_op jit(solution)/shard_map/tf,mf->tm/dot_general | solution.py:60
  1504.3 24.6 %collective-permute-done.61 = bf16[960,1920]{1,0:T(8,128)(2,1)} collective-permute-done((bf16[960,1920]{1,0:T(8,128)(2,1)}, bf16[960,1920]{1,0:T(8,128)(2,1)}, u32[]{:S(2)}, u32[]{:S(2)}) %collective-permute-start.61) | collective-permute-done | bytes 3686432 | tf_op jit(solution)/shard_map/ppermute | solution.py:44
  1533.1 28.8 %collective-permute-done.32 = bf16[960,1920]{1,0:T(8,128)(2,1)} collective-permute-done((bf16[960,1920]{1,0:T(8,128)(2,1)S(1)}, bf16[960,1920]{1,0:T(8,128)(2,1)}, u32[]{:S(2)}, u32[]{:S(2)}) %collective-permute-start.32) | collective-permute-done | bytes 3686432 | tf_op jit(solution)/shard_map/ppermute | solution.py:47
  1590.2 32.2 %collective-permute-done.34 = bf16[960,1920]{1,0:T(8,128)(2,1)S(1)} collective-permute-done((bf16[960,1920]{1,0:T(8,128)(2,1)}, bf16[960,1920]{1,0:T(8,128)(2,1)S(1)}, u32[]{:S(2)}, u32[]{:S(2)}) %collective-permute-start.34) | collective-permute-done | bytes 3686432 | tf_op jit(solution)/shard_map/ppermute | solution.py:44
  (249 shorter events, 273.0 us)
Async XLA Ops:
  163.6 31.9 %collective-permute-start.3 = (bf16[1920,1920]{1,0:T(8,128)(2,1)}, bf16[1920,1920]{1,0:T(8,128)(2,1)}, u32[]{:S(2)}, u32[]{:S(2)}) collective-permute-start(bf16[1920,1920]{1,0:T(8,128)(2,1)} %convolution_convert_fusion.9), channel_id=1, source_target_pairs={{0,1},{1,0},{2,3},{3,2},{4,5},{5,4},{6,7},{7,6}} | collective-permute-start | bytes 22118408 | tf_op jit(solution)/shard_map/ppermute | solution.py:41
  178.3 26.8 %collective-permute-start.4 = (bf16[1920,1920]{1,0:T(8,128)(2,1)}, bf16[1920,1920]{1,0:T(8,128)(2,1)}, u32[]{:S(2)}, u32[]{:S(2)}) collective-permute-start(bf16[1920,1920]{1,0:T(8,128)(2,1)} %convolution_convert_fusion.8), channel_id=1, source_target_pairs={{0,1},{1,0},{2,3},{3,2},{4,5},{5,4},{6,7},{7,6}} | collective-permute-start | bytes 22118408 | tf_op jit(solution)/shard_map/ppermute | solution.py:41
  178.3 83.8 %collective-permute-start.1 = (bf16[1920,1920]{1,0:T(8,128)(2,1)}, bf16[1920,1920]{1,0:T(8,128)(2,1)}, u32[]{:S(2)}, u32[]{:S(2)}) collective-permute-start(bf16[1920,1920]{1,0:T(8,128)(2,1)} %add_convert_fusion.9), channel_id=1, source_target_pairs={{0,2},{1,5},{2,0},{3,7},{4,6},{5,1},{6,4},{7,3}} | collective-permute-start | bytes 22118408 | tf_op jit(solution)/shard_map/ppermute | solution.py:44
  181.3 185.1 %collective-permute-start.5 = (bf16[1920,1920]{1,0:T(8,128)(2,1)}, bf16[1920,1920]{1,0:T(8,128)(2,1)S(1)}, u32[]{:S(2)}, u32[]{:S(2)}) collective-permute-start(bf16[1920,1920]{1,0:T(8,128)(2,1)} %add_convert_fusion.8), channel_id=1, source_target_pairs={{0,2},{1,5},{2,0},{3,7},{4,6},{5,1},{6,4},{7,3}} | collective-permute-start | bytes 22118408 | tf_op jit(solution)/shard_map/ppermute | solution.py:44
  312.0 143.7 %collective-permute-start.14 = (bf16[1920,1920]{1,0:T(8,128)(2,1)}, bf16[1920,1920]{1,0:T(8,128)(2,1)}, u32[]{:S(2)}, u32[]{:S(2)}) collective-permute-start(bf16[1920,1920]{1,0:T(8,128)(2,1)} %convolution_convert_fusion.7), channel_id=1, source_target_pairs={{0,1},{1,0},{2,3},{3,2},{4,5},{5,4},{6,7},{7,6}} | collective-permute-start | bytes 22118408 | tf_op jit(solution)/shard_map/ppermute | solution.py:41
  312.0 69.0 %collective-permute-start.15 = (bf16[960,1920]{1,0:T(8,128)(2,1)}, bf16[960,1920]{1,0:T(8,128)(2,1)}, u32[]{:S(2)}, u32[]{:S(2)}) collective-permute-start(bf16[960,1920]{1,0:T(8,128)(2,1)} %add_convert_fusion.21), channel_id=1, source_target_pairs={{0,4},{1,3},{2,6},{3,1},{4,0},{5,7},{6,2},{7,5}} | collective-permute-start | bytes 11059208 | tf_op jit(solution)/shard_map/ppermute | solution.py:47
  369.6 49.9 %collective-permute-start.6 = (bf16[960,1920]{1,0:T(8,128)(2,1)}, bf16[960,1920]{1,0:T(8,128)(2,1)}, u32[]{:S(2)}, u32[]{:S(2)}) collective-permute-start(bf16[960,1920]{1,0:T(8,128)(2,1)} %add_convert_fusion.20), channel_id=1, source_target_pairs={{0,4},{1,3},{2,6},{3,1},{4,0},{5,7},{6,2},{7,5}} | collective-permute-start | bytes 11059208 | tf_op jit(solution)/shard_map/ppermute | solution.py:47
  379.8 111.1 %collective-permute-start.17 = (bf16[1920,1920]{1,0:T(8,128)(2,1)}, bf16[1920,1920]{1,0:T(8,128)(2,1)}, u32[]{:S(2)}, u32[]{:S(2)}) collective-permute-start(bf16[1920,1920]{1,0:T(8,128)(2,1)} %convolution_convert_fusion.5), channel_id=1, source_target_pairs={{0,1},{1,0},{2,3},{3,2},{4,5},{5,4},{6,7},{7,6}} | collective-permute-start | bytes 22118408 | tf_op jit(solution)/shard_map/ppermute | solution.py:41
  416.8 84.0 %collective-permute-start.40 = (bf16[960,1920]{1,0:T(8,128)(2,1)}, bf16[960,1920]{1,0:T(8,128)(2,1)}, u32[]{:S(2)}, u32[]{:S(2)}) collective-permute-start(bf16[960,1920]{1,0:T(8,128)(2,1)} %get-tuple-element.34), channel_id=1, source_target_pairs={{0,2},{1,5},{2,0},{3,7},{4,6},{5,1},{6,4},{7,3}} | collective-permute-start | bytes 11059208 | tf_op jit(solution)/shard_map/ppermute | solution.py:44
  418.3 83.1 %collective-permute-start.39 = (bf16[960,1920]{1,0:T(8,128)(2,1)}, bf16[960,1920]{1,0:T(8,128)(2,1)}, u32[]{:S(2)}, u32[]{:S(2)}) collective-permute-start(bf16[960,1920]{1,0:T(8,128)(2,1)} %get-tuple-element.34), channel_id=1, source_target_pairs={{0,4},{1,3},{2,6},{3,1},{4,0},{5,7},{6,2},{7,5}} | collective-permute-start | bytes 11059208 | tf_op jit(solution)/shard_map/ppermute | solution.py:47
  419.5 89.5 %collective-permute-start.42 = (bf16[960,1920]{1,0:T(8,128)(2,1)}, bf16[960,1920]{1,0:T(8,128)(2,1)}, u32[]{:S(2)}, u32[]{:S(2)}) collective-permute-start(bf16[960,1920]{1,0:T(8,128)(2,1)} %get-tuple-element.34), channel_id=1, source_target_pairs={{0,1},{1,0},{2,3},{3,2},{4,5},{5,4},{6,7},{7,6}} | collective-permute-start | bytes 11059208 | tf_op jit(solution)/shard_map/ppermute | solution.py:41
  455.8 122.4 %collective-permute-start.8 = (bf16[960,1920]{1,0:T(8,128)(2,1)}, bf16[960,1920]{1,0:T(8,128)(2,1)}, u32[]{:S(2)}, u32[]{:S(2)}) collective-permute-start(bf16[960,1920]{1,0:T(8,128)(2,1)} %get-tuple-element.40), channel_id=1, source_target_pairs={{0,2},{1,5},{2,0},{3,7},{4,6},{5,1},{6,4},{7,3}} | collective-permute-start | bytes 11059208 | tf_op jit(solution)/shard_map/ppermute | solution.py:44
  490.9 89.3 %collective-permute-start.7 = (bf16[960,1920]{1,0:T(8,128)(2,1)}, bf16[960,1920]{1,0:T(8,128)(2,1)}, u32[]{:S(2)}, u32[]{:S(2)}) collective-permute-start(bf16[960,1920]{1,0:T(8,128)(2,1)} %get-tuple-element.40), channel_id=1, source_target_pairs={{0,4},{1,3},{2,6},{3,1},{4,0},{5,7},{6,2},{7,5}} | collective-permute-start | bytes 11059208 | tf_op jit(solution)/shard_map/ppermute | solution.py:47
  500.9 201.0 %collective-permute-start.46 = (bf16[1920,1920]{1,0:T(8,128)(2,1)}, bf16[1920,1920]{1,0:T(8,128)(2,1)}, u32[]{:S(2)}, u32[]{:S(2)}) collective-permute-start(bf16[1920,1920]{1,0:T(8,128)(2,1)} %add_convert_fusion.5), channel_id=1, source_target_pairs={{0,2},{1,5},{2,0},{3,7},{4,6},{5,1},{6,4},{7,3}} | collective-permute-start | bytes 22118408 | tf_op jit(solution)/shard_map/ppermute | solution.py:44
  501.5 201.9 %collective-permute-start.16 = (bf16[1920,1920]{1,0:T(8,128)(2,1)}, bf16[1920,1920]{1,0:T(8,128)(2,1)}, u32[]{:S(2)}, u32[]{:S(2)}) collective-permute-start(bf16[1920,1920]{1,0:T(8,128)(2,1)} %convolution_convert_fusion.6), channel_id=1, source_target_pairs={{0,1},{1,0},{2,3},{3,2},{4,5},{5,4},{6,7},{7,6}} | collective-permute-start | bytes 22118408 | tf_op jit(solution)/shard_map/ppermute | solution.py:41
  509.0 207.7 %collective-permute-start.18 = (bf16[1920,1920]{1,0:T(8,128)(2,1)}, bf16[1920,1920]{1,0:T(8,128)(2,1)}, u32[]{:S(2)}, u32[]{:S(2)}) collective-permute-start(bf16[1920,1920]{1,0:T(8,128)(2,1)} %convolution_convert_fusion.4), channel_id=1, source_target_pairs={{0,1},{1,0},{2,3},{3,2},{4,5},{5,4},{6,7},{7,6}} | collective-permute-start | bytes 22118408 | tf_op jit(solution)/shard_map/ppermute | solution.py:41
  578.2 119.0 %collective-permute-start.41 = (bf16[960,1920]{1,0:T(8,128)(2,1)}, bf16[960,1920]{1,0:T(8,128)(2,1)}, u32[]{:S(2)}, u32[]{:S(2)}) collective-permute-start(bf16[960,1920]{1,0:T(8,128)(2,1)} %collective-permute-done.39), channel_id=1, source_target_pairs={{0,2},{1,5},{2,0},{3,7},{4,6},{5,1},{6,4},{7,3}} | collective-permute-start | bytes 11059208 | tf_op jit(solution)/shard_map/ppermute | solution.py:44
  580.2 121.2 %collective-permute-start.43 = (bf16[960,1920]{1,0:T(8,128)(2,1)}, bf16[960,1920]{1,0:T(8,128)(2,1)}, u32[]{:S(2)}, u32[]{:S(2)}) collective-permute-start(bf16[960,1920]{1,0:T(8,128)(2,1)} %collective-permute-done.39), channel_id=1, source_target_pairs={{0,1},{1,0},{2,3},{3,2},{4,5},{5,4},{6,7},{7,6}} | collective-permute-start | bytes 11059208 | tf_op jit(solution)/shard_map/ppermute | solution.py:41
  697.2 38.6 %collective-permute-start.44 = (bf16[960,1920]{1,0:T(8,128)(2,1)}, bf16[960,1920]{1,0:T(8,128)(2,1)S(1)}, u32[]{:S(2)}, u32[]{:S(2)}) collective-permute-start(bf16[960,1920]{1,0:T(8,128)(2,1)} %collective-permute-done.40), channel_id=1, source_target_pairs={{0,1},{1,0},{2,3},{3,2},{4,5},{5,4},{6,7},{7,6}} | collective-permute-start | bytes 11059208 | tf_op jit(solution)/shard_map/ppermute | solution.py:41
  701.4 37.4 %collective-permute-start.10 = (bf16[960,1920]{1,0:T(8,128)(2,1)}, bf16[960,1920]{1,0:T(8,128)(2,1)}, u32[]{:S(2)}, u32[]{:S(2)}) collective-permute-start(bf16[960,1920]{1,0:T(8,128)(2,1)} %get-tuple-element.40), channel_id=1, source_target_pairs={{0,1},{1,0},{2,3},{3,2},{4,5},{5,4},{6,7},{7,6}} | collective-permute-start | bytes 11059208 | tf_op jit(solution)/shard_map/ppermute | solution.py:41
  701.9 49.4 %collective-permute-start.9 = (bf16[960,1920]{1,0:T(8,128)(2,1)}, bf16[960,1920]{1,0:T(8,128)(2,1)}, u32[]{:S(2)}, u32[]{:S(2)}) collective-permute-start(bf16[960,1920]{1,0:T(8,128)(2,1)} %collective-permute-done.7), channel_id=1, source_target_pairs={{0,2},{1,5},{2,0},{3,7},{4,6},{5,1},{6,4},{7,3}} | collective-permute-start | bytes 11059208 | tf_op jit(solution)/shard_map/ppermute | solution.py:44
  703.4 47.9 %collective-permute-start.45 = (bf16[960,1920]{1,0:T(8,128)(2,1)}, bf16[960,1920]{1,0:T(8,128)(2,1)}, u32[]{:S(2)}, u32[]{:S(2)}) collective-permute-start(bf16[960,1920]{1,0:T(8,128)(2,1)} %collective-permute-done.41), channel_id=1, source_target_pairs={{0,1},{1,0},{2,3},{3,2},{4,5},{5,4},{6,7},{7,6}} | collective-permute-start | bytes 11059208 | tf_op jit(solution)/shard_map/ppermute | solution.py:41
  716.8 169.9 %collective-permute-start.19 = (bf16[1920,1920]{1,0:T(8,128)(2,1)}, bf16[1920,1920]{1,0:T(8,128)(2,1)}, u32[]{:S(2)}, u32[]{:S(2)}) collective-permute-start(bf16[1920,1920]{1,0:T(8,128)(2,1)} %add_convert_fusion.4), channel_id=1, source_target_pairs={{0,2},{1,5},{2,0},{3,7},{4,6},{5,1},{6,4},{7,3}} | collective-permute-start | bytes 22118408 | tf_op jit(solution)/shard_map/ppermute | solution.py:44
  735.8 82.8 %collective-permute-start.47 = (bf16[960,1920]{1,0:T(8,128)(2,1)}, bf16[960,1920]{1,0:T(8,128)(2,1)S(1)}, u32[]{:S(2)}, u32[]{:S(2)}) collective-permute-start(bf16[960,1920]{1,0:T(8,128)(2,1)} %add_convert_fusion.13), channel_id=1, source_target_pairs={{0,4},{1,3},{2,6},{3,1},{4,0},{5,7},{6,2},{7,5}} | collective-permute-start | bytes 11059208 | tf_op jit(solution)/shard_map/ppermute | solution.py:47
  738.7 98.7 %collective-permute-start.11 = (bf16[960,1920]{1,0:T(8,128)(2,1)}, bf16[960,1920]{1,0:T(8,128)(2,1)}, u32[]{:S(2)}, u32[]{:S(2)}) collective-permute-start(bf16[960,1920]{1,0:T(8,128)(2,1)} %collective-permute-done.7), channel_id=1, source_target_pairs={{0,1},{1,0},{2,3},{3,2},{4,5},{5,4},{6,7},{7,6}} | collective-permute-start | bytes 11059208 | tf_op jit(solution)/shard_map/ppermute | solution.py:41
  751.3 85.7 %collective-permute-start.12 = (bf16[960,1920]{1,0:T(8,128)(2,1)}, bf16[960,1920]{1,0:T(8,128)(2,1)}, u32[]{:S(2)}, u32[]{:S(2)}) collective-permute-start(bf16[960,1920]{1,0:T(8,128)(2,1)} %collective-permute-done.8), channel_id=1, source_target_pairs={{0,1},{1,0},{2,3},{3,2},{4,5},{5,4},{6,7},{7,6}} | collective-permute-start | bytes 11059208 | tf_op jit(solution)/shard_map/ppermute | solution.py:41
  751.3 87.0 %collective-permute-start.13 = (bf16[960,1920]{1,0:T(8,128)(2,1)}, bf16[960,1920]{1,0:T(8,128)(2,1)}, u32[]{:S(2)}, u32[]{:S(2)}) collective-permute-start(bf16[960,1920]{1,0:T(8,128)(2,1)} %collective-permute-done.9), channel_id=1, source_target_pairs={{0,1},{1,0},{2,3},{3,2},{4,5},{5,4},{6,7},{7,6}} | collective-permute-start | bytes 11059208 | tf_op jit(solution)/shard_map/ppermute | solution.py:41
  818.6 129.4 %collective-permute-start.56 = (bf16[1920,1920]{1,0:T(8,128)(2,1)}, bf16[1920,1920]{1,0:T(8,128)(2,1)}, u32[]{:S(2)}, u32[]{:S(2)}) collective-permute-start(bf16[1920,1920]{1,0:T(8,128)(2,1)} %convolution_convert_fusion), channel_id=1, source_target_pairs={{0,1},{1,0},{2,3},{3,2},{4,5},{5,4},{6,7},{7,6}} | collective-permute-start | bytes 22118408 | tf_op jit(solution)/shard_map/ppermute | solution.py:41
  837.0 135.6 %collective-permute-start.55 = (bf16[1920,1920]{1,0:T(8,128)(2,1)}, bf16[1920,1920]{1,0:T(8,128)(2,1)}, u32[]{:S(2)}, u32[]{:S(2)}) collective-permute-start(bf16[1920,1920]{1,0:T(8,128)(2,1)} %convolution_convert_fusion.1), channel_id=1, source_target_pairs={{0,1},{1,0},{2,3},{3,2},{4,5},{5,4},{6,7},{7,6}} | collective-permute-start | bytes 22118408 | tf_op jit(solution)/shard_map/ppermute | solution.py:41
  837.5 105.3 %collective-permute-start.49 = (bf16[960,1920]{1,0:T(8,128)(2,1)}, bf16[960,1920]{1,0:T(8,128)(2,1)}, u32[]{:S(2)}, u32[]{:S(2)}) collective-permute-start(bf16[960,1920]{1,0:T(8,128)(2,1)} %get-tuple-element.32), channel_id=1, source_target_pairs={{0,2},{1,5},{2,0},{3,7},{4,6},{5,1},{6,4},{7,3}} | collective-permute-start | bytes 11059208 | tf_op jit(solution)/shard_map/ppermute | solution.py:44
  838.3 104.4 %collective-permute-start.48 = (bf16[960,1920]{1,0:T(8,128)(2,1)}, bf16[960,1920]{1,0:T(8,128)(2,1)}, u32[]{:S(2)}, u32[]{:S(2)}) collective-permute-start(bf16[960,1920]{1,0:T(8,128)(2,1)} %get-tuple-element.32), channel_id=1, source_target_pairs={{0,4},{1,3},{2,6},{3,1},{4,0},{5,7},{6,2},{7,5}} | collective-permute-start | bytes 11059208 | tf_op jit(solution)/shard_map/ppermute | solution.py:47
  886.6 72.0 %collective-permute-start.51 = (bf16[960,1920]{1,0:T(8,128)(2,1)}, bf16[960,1920]{1,0:T(8,128)(2,1)}, u32[]{:S(2)}, u32[]{:S(2)}) collective-permute-start(bf16[960,1920]{1,0:T(8,128)(2,1)} %get-tuple-element.32), channel_id=1, source_target_pairs={{0,1},{1,0},{2,3},{3,2},{4,5},{5,4},{6,7},{7,6}} | collective-permute-start | bytes 11059208 | tf_op jit(solution)/shard_map/ppermute | solution.py:41
  942.8 104.4 %collective-permute-start.28 = (bf16[1920,1920]{1,0:T(8,128)(2,1)}, bf16[1920,1920]{1,0:T(8,128)(2,1)}, u32[]{:S(2)}, u32[]{:S(2)}) collective-permute-start(bf16[1920,1920]{1,0:T(8,128)(2,1)} %fusion.84), channel_id=1, source_target_pairs={{0,1},{1,0},{2,3},{3,2},{4,5},{5,4},{6,7},{7,6}} | collective-permute-start | bytes 22118408 | tf_op jit(solution)/shard_map/ppermute | solution.py:41
  942.8 104.4 %collective-permute-start.29 = (bf16[1920,1920]{1,0:T(8,128)(2,1)}, bf16[1920,1920]{1,0:T(8,128)(2,1)}, u32[]{:S(2)}, u32[]{:S(2)}) collective-permute-start(bf16[1920,1920]{1,0:T(8,128)(2,1)} %fusion.85), channel_id=1, source_target_pairs={{0,1},{1,0},{2,3},{3,2},{4,5},{5,4},{6,7},{7,6}} | collective-permute-start | bytes 22118408 | tf_op jit(solution)/shard_map/ppermute | solution.py:41
  948.0 73.5 %collective-permute-start.20 = (bf16[960,1920]{1,0:T(8,128)(2,1)}, bf16[960,1920]{1,0:T(8,128)(2,1)}, u32[]{:S(2)}, u32[]{:S(2)}) collective-permute-start(bf16[960,1920]{1,0:T(8,128)(2,1)} %add_convert_fusion.17), channel_id=1, source_target_pairs={{0,4},{1,3},{2,6},{3,1},{4,0},{5,7},{6,2},{7,5}} | collective-permute-start | bytes 11059208 | tf_op jit(solution)/shard_map/ppermute | solution.py:47
  958.6 199.9 %collective-permute-start.57 = (bf16[1920,1920]{1,0:T(8,128)(2,1)}, bf16[1920,1920]{1,0:T(8,128)(2,1)}, u32[]{:S(2)}, u32[]{:S(2)}) collective-permute-start(bf16[1920,1920]{1,0:T(8,128)(2,1)} %add_convert_fusion), channel_id=1, source_target_pairs={{0,2},{1,5},{2,0},{3,7},{4,6},{5,1},{6,4},{7,3}} | collective-permute-start | bytes 22118408 | tf_op jit(solution)/shard_map/ppermute | solution.py:44
  972.6 85.5 %collective-permute-start.53 = (bf16[960,1920]{1,0:T(8,128)(2,1)}, bf16[960,1920]{1,0:T(8,128)(2,1)}, u32[]{:S(2)}, u32[]{:S(2)}) collective-permute-start(bf16[960,1920]{1,0:T(8,128)(2,1)} %collective-permute-done.49), channel_id=1, source_target_pairs={{0,1},{1,0},{2,3},{3,2},{4,5},{5,4},{6,7},{7,6}} | collective-permute-start | bytes 11059208 | tf_op jit(solution)/shard_map/ppermute | solution.py:41
  1021.5 127.0 %collective-permute-start.50 = (bf16[960,1920]{1,0:T(8,128)(2,1)}, bf16[960,1920]{1,0:T(8,128)(2,1)}, u32[]{:S(2)}, u32[]{:S(2)}) collective-permute-start(bf16[960,1920]{1,0:T(8,128)(2,1)} %collective-permute-done.48), channel_id=1, source_target_pairs={{0,2},{1,5},{2,0},{3,7},{4,6},{5,1},{6,4},{7,3}} | collective-permute-start | bytes 11059208 | tf_op jit(solution)/shard_map/ppermute | solution.py:44
  1047.2 130.8 %collective-permute-start.52 = (bf16[960,1920]{1,0:T(8,128)(2,1)}, bf16[960,1920]{1,0:T(8,128)(2,1)S(1)}, u32[]{:S(2)}, u32[]{:S(2)}) collective-permute-start(bf16[960,1920]{1,0:T(8,128)(2,1)} %collective-permute-done.48), channel_id=1, source_target_pairs={{0,1},{1,0},{2,3},{3,2},{4,5},{5,4},{6,7},{7,6}} | collective-permute-start | bytes 11059208 | tf_op jit(solution)/shard_map/ppermute | solution.py:41
  1047.2 136.4 %collective-permute-start.21 = (bf16[960,1920]{1,0:T(8,128)(2,1)S(1)}, bf16[960,1920]{1,0:T(8,128)(2,1)}, u32[]{:S(2)}, u32[]{:S(2)}) collective-permute-start(bf16[960,1920]{1,0:T(8,128)(2,1)S(1)} %get-tuple-element.38), channel_id=1, source_target_pairs={{0,4},{1,3},{2,6},{3,1},{4,0},{5,7},{6,2},{7,5}} | collective-permute-start | bytes 11059208 | tf_op jit(solution)/shard_map/ppermute | solution.py:47
  1058.0 268.5 %collective-permute-start.30 = (bf16[1920,1920]{1,0:T(8,128)(2,1)}, bf16[1920,1920]{1,0:T(8,128)(2,1)S(1)}, u32[]{:S(2)}, u32[]{:S(2)}) collective-permute-start(bf16[1920,1920]{1,0:T(8,128)(2,1)} %fusion.26), channel_id=1, source_target_pairs={{0,2},{1,5},{2,0},{3,7},{4,6},{5,1},{6,4},{7,3}} | collective-permute-start | bytes 22118408 | tf_op jit(solution)/shard_map/ppermute | solution.py:44
  1148.5 39.8 %collective-permute-start.54 = (bf16[960,1920]{1,0:T(8,128)(2,1)}, bf16[960,1920]{1,0:T(8,128)(2,1)}, u32[]{:S(2)}, u32[]{:S(2)}) collective-permute-start(bf16[960,1920]{1,0:T(8,128)(2,1)} %collective-permute-done.50), channel_id=1, source_target_pairs={{0,1},{1,0},{2,3},{3,2},{4,5},{5,4},{6,7},{7,6}} | collective-permute-start | bytes 11059208 | tf_op jit(solution)/shard_map/ppermute | solution.py:41
  1158.5 148.0 %collective-permute-start.22 = (bf16[960,1920]{1,0:T(8,128)(2,1)S(1)}, bf16[960,1920]{1,0:T(8,128)(2,1)}, u32[]{:S(2)}, u32[]{:S(2)}) collective-permute-start(bf16[960,1920]{1,0:T(8,128)(2,1)S(1)} %get-tuple-element.38), channel_id=1, source_target_pairs={{0,2},{1,5},{2,0},{3,7},{4,6},{5,1},{6,4},{7,3}} | collective-permute-start | bytes 11059208 | tf_op jit(solution)/shard_map/ppermute | solution.py:44
  1178.0 139.9 %collective-permute-start.58 = (bf16[960,1920]{1,0:T(8,128)(2,1)S(1)}, bf16[960,1920]{1,0:T(8,128)(2,1)}, u32[]{:S(2)}, u32[]{:S(2)}) collective-permute-start(bf16[960,1920]{1,0:T(8,128)(2,1)S(1)} %add_convert_fusion.11), channel_id=1, source_target_pairs={{0,4},{1,3},{2,6},{3,1},{4,0},{5,7},{6,2},{7,5}} | collective-permute-start | bytes 11059208 | tf_op jit(solution)/shard_map/ppermute | solution.py:47
  1183.6 178.4 %collective-permute-start.23 = (bf16[960,1920]{1,0:T(8,128)(2,1)}, bf16[960,1920]{1,0:T(8,128)(2,1)}, u32[]{:S(2)}, u32[]{:S(2)}) collective-permute-start(bf16[960,1920]{1,0:T(8,128)(2,1)} %collective-permute-done.21), channel_id=1, source_target_pairs={{0,2},{1,5},{2,0},{3,7},{4,6},{5,1},{6,4},{7,3}} | collective-permute-start | bytes 11059208 | tf_op jit(solution)/shard_map/ppermute | solution.py:44
  1188.3 182.3 %collective-permute-start.24 = (bf16[960,1920]{1,0:T(8,128)(2,1)S(1)}, bf16[960,1920]{1,0:T(8,128)(2,1)}, u32[]{:S(2)}, u32[]{:S(2)}) collective-permute-start(bf16[960,1920]{1,0:T(8,128)(2,1)S(1)} %get-tuple-element.38), channel_id=1, source_target_pairs={{0,1},{1,0},{2,3},{3,2},{4,5},{5,4},{6,7},{7,6}} | collective-permute-start | bytes 11059208 | tf_op jit(solution)/shard_map/ppermute | solution.py:41
  1306.5 69.7 %collective-permute-start.25 = (bf16[960,1920]{1,0:T(8,128)(2,1)}, bf16[960,1920]{1,0:T(8,128)(2,1)}, u32[]{:S(2)}, u32[]{:S(2)}) collective-permute-start(bf16[960,1920]{1,0:T(8,128)(2,1)} %collective-permute-done.21), channel_id=1, source_target_pairs={{0,1},{1,0},{2,3},{3,2},{4,5},{5,4},{6,7},{7,6}} | collective-permute-start | bytes 11059208 | tf_op jit(solution)/shard_map/ppermute | solution.py:41
  1317.9 72.2 %collective-permute-start.26 = (bf16[960,1920]{1,0:T(8,128)(2,1)}, bf16[960,1920]{1,0:T(8,128)(2,1)}, u32[]{:S(2)}, u32[]{:S(2)}) collective-permute-start(bf16[960,1920]{1,0:T(8,128)(2,1)} %collective-permute-done.22), channel_id=1, source_target_pairs={{0,1},{1,0},{2,3},{3,2},{4,5},{5,4},{6,7},{7,6}} | collective-permute-start | bytes 11059208 | tf_op jit(solution)/shard_map/ppermute | solution.py:41
  1326.5 67.7 %collective-permute-start.59 = (bf16[960,1920]{1,0:T(8,128)(2,1)}, bf16[960,1920]{1,0:T(8,128)(2,1)}, u32[]{:S(2)}, u32[]{:S(2)}) collective-permute-start(bf16[960,1920]{1,0:T(8,128)(2,1)} %get-tuple-element.30), channel_id=1, source_target_pairs={{0,4},{1,3},{2,6},{3,1},{4,0},{5,7},{6,2},{7,5}} | collective-permute-start | bytes 11059208 | tf_op jit(solution)/shard_map/ppermute | solution.py:47
  1362.0 34.4 %collective-permute-start.27 = (bf16[960,1920]{1,0:T(8,128)(2,1)}, bf16[960,1920]{1,0:T(8,128)(2,1)S(1)}, u32[]{:S(2)}, u32[]{:S(2)}) collective-permute-start(bf16[960,1920]{1,0:T(8,128)(2,1)} %collective-permute-done.23), channel_id=1, source_target_pairs={{0,1},{1,0},{2,3},{3,2},{4,5},{5,4},{6,7},{7,6}} | collective-permute-start | bytes 11059208 | tf_op jit(solution)/shard_map/ppermute | solution.py:41
  1370.6 102.3 %collective-permute-start.31 = (bf16[960,1920]{1,0:T(8,128)(2,1)S(1)}, bf16[960,1920]{1,0:T(8,128)(2,1)}, u32[]{:S(2)}, u32[]{:S(2)}) collective-permute-start(bf16[960,1920]{1,0:T(8,128)(2,1)S(1)} %add_convert_fusion.15), channel_id=1, source_target_pairs={{0,4},{1,3},{2,6},{3,1},{4,0},{5,7},{6,2},{7,5}} | collective-permute-start | bytes 11059208 | tf_op jit(solution)/shard_map/ppermute | solution.py:47
  1376.2 107.0 %collective-permute-start.60 = (bf16[960,1920]{1,0:T(8,128)(2,1)}, bf16[960,1920]{1,0:T(8,128)(2,1)}, u32[]{:S(2)}, u32[]{:S(2)}) collective-permute-start(bf16[960,1920]{1,0:T(8,128)(2,1)} %get-tuple-element.30), channel_id=1, source_target_pairs={{0,2},{1,5},{2,0},{3,7},{4,6},{5,1},{6,4},{7,3}} | collective-permute-start | bytes 11059208 | tf_op jit(solution)/shard_map/ppermute | solution.py:44
  1394.3 134.6 %collective-permute-start.61 = (bf16[960,1920]{1,0:T(8,128)(2,1)}, bf16[960,1920]{1,0:T(8,128)(2,1)}, u32[]{:S(2)}, u32[]{:S(2)}) collective-permute-start(bf16[960,1920]{1,0:T(8,128)(2,1)} %collective-permute-done.59), channel_id=1, source_target_pairs={{0,2},{1,5},{2,0},{3,7},{4,6},{5,1},{6,4},{7,3}} | collective-permute-start | bytes 11059208 | tf_op jit(solution)/shard_map/ppermute | solution.py:44
  1479.2 82.7 %collective-permute-start.32 = (bf16[960,1920]{1,0:T(8,128)(2,1)S(1)}, bf16[960,1920]{1,0:T(8,128)(2,1)}, u32[]{:S(2)}, u32[]{:S(2)}) collective-permute-start(bf16[960,1920]{1,0:T(8,128)(2,1)S(1)} %get-tuple-element.36), channel_id=1, source_target_pairs={{0,4},{1,3},{2,6},{3,1},{4,0},{5,7},{6,2},{7,5}} | collective-permute-start | bytes 11059208 | tf_op jit(solution)/shard_map/ppermute | solution.py:47
  1480.7 91.9 %collective-permute-start.62 = (bf16[960,1920]{1,0:T(8,128)(2,1)}, bf16[960,1920]{1,0:T(8,128)(2,1)}, u32[]{:S(2)}, u32[]{:S(2)}) collective-permute-start(bf16[960,1920]{1,0:T(8,128)(2,1)} %get-tuple-element.30), channel_id=1, source_target_pairs={{0,1},{1,0},{2,3},{3,2},{4,5},{5,4},{6,7},{7,6}} | collective-permute-start | bytes 11059208 | tf_op jit(solution)/shard_map/ppermute | solution.py:41
  1480.7 102.2 %collective-permute-start.33 = (bf16[960,1920]{1,0:T(8,128)(2,1)S(1)}, bf16[960,1920]{1,0:T(8,128)(2,1)}, u32[]{:S(2)}, u32[]{:S(2)}) collective-permute-start(bf16[960,1920]{1,0:T(8,128)(2,1)S(1)} %get-tuple-element.36), channel_id=1, source_target_pairs={{0,2},{1,5},{2,0},{3,7},{4,6},{5,1},{6,4},{7,3}} | collective-permute-start | bytes 11059208 | tf_op jit(solution)/shard_map/ppermute | solution.py:44
  1483.2 93.6 %collective-permute-start.64 = (bf16[960,1920]{1,0:T(8,128)(2,1)}, bf16[960,1920]{1,0:T(8,128)(2,1)}, u32[]{:S(2)}, u32[]{:S(2)}) collective-permute-start(bf16[960,1920]{1,0:T(8,128)(2,1)} %collective-permute-done.60), channel_id=1, source_target_pairs={{0,1},{1,0},{2,3},{3,2},{4,5},{5,4},{6,7},{7,6}} | collective-permute-start | bytes 11059208 | tf_op jit(solution)/shard_map/ppermute | solution.py:41
  1528.9 59.2 %collective-permute-start.63 = (bf16[960,1920]{1,0:T(8,128)(2,1)}, bf16[960,1920]{1,0:T(8,128)(2,1)S(1)}, u32[]{:S(2)}, u32[]{:S(2)}) collective-permute-start(bf16[960,1920]{1,0:T(8,128)(2,1)} %collective-permute-done.59), channel_id=1, source_target_pairs={{0,1},{1,0},{2,3},{3,2},{4,5},{5,4},{6,7},{7,6}} | collective-permute-start | bytes 11059208 | tf_op jit(solution)/shard_map/ppermute | solution.py:41
  1561.9 60.5 %collective-permute-start.34 = (bf16[960,1920]{1,0:T(8,128)(2,1)}, bf16[960,1920]{1,0:T(8,128)(2,1)S(1)}, u32[]{:S(2)}, u32[]{:S(2)}) collective-permute-start(bf16[960,1920]{1,0:T(8,128)(2,1)} %collective-permute-done.32), channel_id=1, source_target_pairs={{0,2},{1,5},{2,0},{3,7},{4,6},{5,1},{6,4},{7,3}} | collective-permute-start | bytes 11059208 | tf_op jit(solution)/shard_map/ppermute | solution.py:44
  1572.6 56.7 %collective-permute-start.65 = (bf16[960,1920]{1,0:T(8,128)(2,1)}, bf16[960,1920]{1,0:T(8,128)(2,1)S(1)}, u32[]{:S(2)}, u32[]{:S(2)}) collective-permute-start(bf16[960,1920]{1,0:T(8,128)(2,1)} %collective-permute-done.61), channel_id=1, source_target_pairs={{0,1},{1,0},{2,3},{3,2},{4,5},{5,4},{6,7},{7,6}} | collective-permute-start | bytes 11059208 | tf_op jit(solution)/shard_map/ppermute | solution.py:41
  1576.8 54.7 %collective-permute-start.35 = (bf16[960,1920]{1,0:T(8,128)(2,1)S(1)}, bf16[960,1920]{1,0:T(8,128)(2,1)S(1)}, u32[]{:S(2)}, u32[]{:S(2)}) collective-permute-start(bf16[960,1920]{1,0:T(8,128)(2,1)S(1)} %get-tuple-element.36), channel_id=1, source_target_pairs={{0,1},{1,0},{2,3},{3,2},{4,5},{5,4},{6,7},{7,6}} | collective-permute-start | bytes 11059208 | tf_op jit(solution)/shard_map/ppermute | solution.py:41
  1583.0 50.6 %collective-permute-start.36 = (bf16[960,1920]{1,0:T(8,128)(2,1)}, bf16[960,1920]{1,0:T(8,128)(2,1)S(1)}, u32[]{:S(2)}, u32[]{:S(2)}) collective-permute-start(bf16[960,1920]{1,0:T(8,128)(2,1)} %collective-permute-done.32), channel_id=1, source_target_pairs={{0,1},{1,0},{2,3},{3,2},{4,5},{5,4},{6,7},{7,6}} | collective-permute-start | bytes 11059208 | tf_op jit(solution)/shard_map/ppermute | solution.py:41
  1588.1 47.6 %collective-permute-start.37 = (bf16[960,1920]{1,0:T(8,128)(2,1)}, bf16[960,1920]{1,0:T(8,128)(2,1)S(1)}, u32[]{:S(2)}, u32[]{:S(2)}) collective-permute-start(bf16[960,1920]{1,0:T(8,128)(2,1)} %collective-permute-done.33), channel_id=1, source_target_pairs={{0,1},{1,0},{2,3},{3,2},{4,5},{5,4},{6,7},{7,6}} | collective-permute-start | bytes 11059208 | tf_op jit(solution)/shard_map/ppermute | solution.py:41
  1622.4 15.5 collective-permute-start.38
  (39 other events, 1438.1 us)
